TPU v7x, 32 devices: a whole 2x2x4 slice. The times are simulated.
32 devices in a mesh: rep: 8 (over z, core), tp: 4 (over y, x).
Axes of the slice: x: 2, y: 2, z: 4, core: 2. Of those that a mesh axis runs over, the one named last changes fastest.
Arguments:
- hidden_state: bfloat16 [32, 3584], P('rep'), may hold values from -6 to 6
- lengths: int32 [32], P('rep'), may hold values from 1 to 2048, as said below
- old_qkv: bfloat16 [3584, 4608], P(None, 'tp'), may hold values from -0.09375 to 0.09375
- old_out: bfloat16 [3584, 3584], P(None, 'tp'), may hold values from -0.09375 to 0.09375
- cache_keys: bfloat16 [32, 2048, 512], P('rep', 'tp'), may hold values from -64 to 64
- cache_values: bfloat16 [32, 2048, 512], P('rep', 'tp'), may hold values from -6 to 6
- new_qkv: bfloat16 [3584, 4608], P(('rep', 'tp')), may hold values from -0.09375 to 0.09375
- new_out: bfloat16 [3584, 3584], P(('rep', 'tp')), may hold values from -0.09375 to 0.09375
Outputs:
- decoded: bfloat16 [32, 3584], P('rep', 'tp')
- resharded_qkv: bfloat16 [3584, 4608], P(None, 'tp')
- resharded_out: bfloat16 [3584, 3584], P(None, 'tp')
Inputs may be any that keep to these rules, and one draw needn't show every extreme that they name: Every sequence has 1 to 2048 cached tokens, held in positions 0 to lengths - 1; in every draw some sequence fills its cache.
All inputs are finite; a program needn't handle non-finite values.
Results may differ from a plain program's by a relative error of at most 0.012.
Values may be sent and summed in bfloat16 or wider, within the bound.
A program may use at most 128 MiB of HBM per device.

v0:
```python
import functools

import jax
import jax.numpy as jnp
import numpy as np
from jax import lax
from jax.experimental import pallas as pl
from jax.experimental.pallas import tpu as pltpu
from jax.sharding import PartitionSpec as P

HQ = 28
KVH = 4
HD = 128
PAD = 8
CUTS = 8
VMEM_BYTES = 67043328
SLACK = 600000
MESH = pl.DeviceIdType.MESH


ROPE_BASE = 1000000.0


def rotate(vectors, positions):
    half_dim = vectors.shape[-1] // 2
    frequency = ROPE_BASE ** (-2.0 * jnp.arange(half_dim, dtype=jnp.float32) / (2 * half_dim))
    angles = positions.astype(jnp.float32)[:, None, None] * frequency
    first_half = vectors[..., :half_dim]
    second_half = vectors[..., half_dim:]
    return jnp.concatenate(
        [
            first_half * jnp.cos(angles) - second_half * jnp.sin(angles),
            second_half * jnp.cos(angles) + first_half * jnp.sin(angles),
        ],
        axis=-1,
    )


def per_device(hidden_state, lengths, old_qkv, old_out, cache_keys, cache_values):
    seq_count = hidden_state.shape[0]
    local_joined = jnp.dot(hidden_state, old_qkv, preferred_element_type=jnp.float32).astype(
        jnp.bfloat16
    )
    joined_rows = lax.all_gather(local_joined, "tp", axis=1, tiled=True)
    q_width = HQ * HD
    k_width = KVH * HD
    group_size = HQ // KVH
    queries = rotate(
        joined_rows[:, :q_width].astype(jnp.float32).reshape(seq_count, HQ, HD), lengths
    ).astype(jnp.bfloat16)
    own_keys = rotate(
        joined_rows[:, q_width : q_width + k_width].astype(jnp.float32).reshape(seq_count, KVH, HD),
        lengths,
    ).astype(jnp.bfloat16)
    own_values = joined_rows[:, q_width + k_width :].reshape(seq_count, KVH, HD)
    inv_root = 1.0 / jnp.sqrt(jnp.float32(HD))
    cache_rows = cache_keys.shape[1]
    grouped = queries.reshape(seq_count, KVH, group_size, HD)
    key_blocks = cache_keys.reshape(seq_count, cache_rows, KVH, HD)
    value_blocks = cache_values.reshape(seq_count, cache_rows, KVH, HD)
    scores = (
        jnp.einsum("skgd,stkd->skgt", grouped, key_blocks, preferred_element_type=jnp.float32)
        * inv_root
    )
    positions = lax.axis_index("tp") * cache_rows + jnp.arange(cache_rows, dtype=jnp.int32)
    live_mask = (positions[None, :] < lengths[:, None])[:, None, None, :]
    scores = jnp.where(live_mask, scores, jnp.float32(-1e30))
    own_score = (
        jnp.sum(grouped.astype(jnp.float32) * own_keys.astype(jnp.float32)[:, :, None, :], axis=-1)
        * inv_root
    )
    local_top = jnp.maximum(jnp.max(scores, axis=-1), own_score)
    top_score = lax.pmax(local_top, "tp")
    weights = jnp.where(live_mask, jnp.exp(scores - top_score[..., None]), jnp.float32(0.0)).astype(
        jnp.bfloat16
    )
    numer_part = jnp.einsum(
        "skgt,stkd->skgd", weights, value_blocks, preferred_element_type=jnp.float32
    )
    denom_part = jnp.sum(weights.astype(jnp.float32), axis=-1)
    numerator, denominator = lax.psum((numer_part, denom_part), "tp")
    own_weight = lax.optimization_barrier(
        jnp.exp(own_score - top_score).astype(jnp.bfloat16)
    ).astype(jnp.float32)
    numerator = numerator + own_weight[..., None] * own_values.astype(jnp.float32)[:, :, None, :]
    denominator = denominator + own_weight
    attended = (numerator / denominator[..., None]).reshape(seq_count, q_width).astype(jnp.bfloat16)
    decoded = jnp.dot(attended, old_out, preferred_element_type=jnp.float32).astype(jnp.bfloat16)
    return decoded


def native_move(new_qkv, new_out):
    def move(block):
        piece = lax.all_to_all(block, "tp", split_axis=1, concat_axis=0, tiled=True)
        return lax.all_gather(piece, "rep", axis=0, tiled=True)

    return move(new_qkv), move(new_out)


def flip(index, bits, size):
    out = index
    bit = 1
    while bit < size:
        if (bits // bit) % 2:
            out = out + bit - 2 * bit * ((index // bit) % 2)
        bit *= 2
    return out


def step_kernel(
    planes, tps,
    hidden, lengths, frequency, old_qkv, old_out, keys, values, new_qkv, new_out,
    decoded, qkv_full, out_full,
    a_send, a_recv, u_send, u_recv, d_send, d_recv, s_send, s_recv, own_sem, load_sem,
    j_send, j_recv, n_send, n_recv,
    w_qkv, w_out, k_held, v_held, joined, rotated, own_score, own_value, parts, attended,
    cosine, sine,
):
    rep, tp = lax.axis_index("rep"), lax.axis_index("tp")
    plane, core = rep // 2, rep % 2
    rows = new_qkv.shape[0]
    blocks, fulls = (new_qkv, new_out), (qkv_full, out_full)
    widths = (qkv_full.shape[1], out_full.shape[1])
    up = (jnp.minimum(plane + 1, planes - 1) * 2 + core, tp)
    down = (jnp.maximum(plane - 1, 0) * 2 + core, tp)
    twin = (plane * 2 + 1 - core, tp)
    peers = [(rep, flip(tp, k, tps)) for k in range(1, tps)]
    can_up, can_down = plane < planes - 1, plane > 0

    barrier = pltpu.get_barrier_semaphore()
    for device in [twin] + peers:
        pl.semaphore_signal(barrier, inc=1, device_id=device, device_id_type=MESH)

    @pl.when(can_up)
    def _():
        pl.semaphore_signal(barrier, inc=1, device_id=up, device_id_type=MESH)

    @pl.when(can_down)
    def _():
        pl.semaphore_signal(barrier, inc=1, device_id=down, device_id_type=MESH)

    @pl.when(can_up & can_down)
    def _():
        pl.semaphore_wait(barrier, tps + 2)

    @pl.when(jnp.logical_not(can_up & can_down))
    def _():
        pl.semaphore_wait(barrier, tps + 1)

    def remote(source, target, send, recv, device):
        return pltpu.make_async_remote_copy(
            src_ref=source, dst_ref=target, send_sem=send, recv_sem=recv,
            device_id=device, device_id_type=MESH,
        )

    def rows_of(source_plane, source_core, k, w):
        start = ((source_plane * 2 + source_core) * tps + flip(tp, k, tps)) * rows
        return fulls[w].at[pl.ds(pl.multiple_of(start, rows), rows)]

    def column(w, t):
        return blocks[w].at[:, pl.ds(pl.multiple_of(t * widths[w], 128), widths[w])]

    def in_plane(k, w):
        return remote(
            column(w, flip(tp, k, tps)), rows_of(plane, core, 0, w),
            a_send.at[k, w], a_recv.at[k, w], peers[k - 1],
        )

    def piece(d, k, w):
        target = rows_of(plane - d, core, k, w)
        return target, (column(w, tp) if d == 0 and k == 0 else target)

    def to_up(d, k, w):
        target, source = piece(d, k, w)
        return remote(source, target, u_send.at[d, k, w], u_recv.at[d, k, w], up)

    def to_down(d, k, w):
        target, source = piece(-d, k, w)
        return remote(source, target, d_send.at[d, k, w], d_recv.at[d, k, w], down)

    def to_twin(d, k, w):
        target, source = piece(d, k, w)
        slot = d + planes - 1
        return remote(source, target, s_send.at[slot, k, w], s_recv.at[slot, k, w], twin)

    def own(k, w):
        @pl.when(can_up)
        def _():
            to_up(0, k, w).start()

        @pl.when(can_down)
        def _():
            to_down(0, k, w).start()

        to_twin(0, k, w).start()

    def relay(d):
        for k in range(tps):
            for w in range(2):

                @pl.when(plane >= d)
                def _():
                    target = rows_of(plane - d, core, k, w)
                    remote(
                        target, target, u_send.at[d - 1, k, w], u_recv.at[d - 1, k, w], up
                    ).wait_recv()

                    @pl.when(can_up)
                    def _():
                        to_up(d, k, w).start()

                    to_twin(d, k, w).start()

                @pl.when(plane + d < planes)
                def _():
                    target = rows_of(plane + d, core, k, w)
                    remote(
                        target, target, d_send.at[d - 1, k, w], d_recv.at[d - 1, k, w], down
                    ).wait_recv()

                    @pl.when(can_down)
                    def _():
                        to_down(d, k, w).start()

                    to_twin(-d, k, w).start()

    for k in range(1, tps):
        for w in range(2):
            in_plane(k, w).start()
    for w in range(2):
        own(0, w)
    locals_ = [
        pltpu.make_async_copy(column(w, tp), rows_of(plane, core, 0, w), own_sem.at[w])
        for w in range(2)
    ]
    loads = [
        pltpu.make_async_copy(source, target, load_sem.at[i])
        for i, (source, target) in enumerate(
            ((old_qkv, w_qkv), (keys, k_held), (values, v_held), (old_out, w_out))
        )
    ]
    for copy in locals_ + loads:
        copy.start()
    for k in range(1, tps):
        for w in range(2):
            target = rows_of(plane, core, k, w)
            remote(
                target, target, a_send.at[k, w], a_recv.at[k, w], peers[k - 1]
            ).wait_recv()
            own(k, w)

    seqs = hidden.shape[0]
    lane = lax.broadcasted_iota(jnp.int32, (1, HD), 1)
    for s in range(seqs):
        angles = lengths[s].astype(jnp.float32) * frequency[...]
        cosine[s : s + 1, :] = jnp.cos(angles)
        sine[s : s + 1, :] = jnp.where(lane < HD // 2, -jnp.sin(angles), jnp.sin(angles))
    tile = 128
    loads[0].wait()

    @pl.loop(0, w_qkv.shape[1] // tile)
    def _(i):
        at = pl.ds(pl.multiple_of(i * tile, tile), tile)
        joined[tp, :, at] = jnp.dot(
            hidden[...], w_qkv[:, at], preferred_element_type=jnp.float32
        ).astype(joined.dtype)

    def send_joined(k):
        return remote(
            joined.at[tp], joined.at[tp], j_send.at[k], j_recv.at[k], peers[k - 1]
        )

    for k in range(1, tps):
        send_joined(k).start()

    relay(1)

    for k in range(1, tps):
        slot = joined.at[flip(tp, k, tps)]
        remote(slot, slot, j_send.at[k], j_recv.at[k], peers[k - 1]).wait_recv()
    for copy in loads[1:]:
        copy.wait()

    group = HQ // KVH
    positions = k_held.shape[1]
    per_slot = joined.shape[2] // HD
    inv_root = 1.0 / jnp.sqrt(jnp.float32(HD))

    def head(j):
        at = (j % per_slot) * HD
        return joined[j // per_slot, :, at : at + HD].astype(jnp.float32)

    def turn(v):
        swapped = jnp.concatenate([v[:, HD // 2 :], v[:, : HD // 2]], axis=1)
        return (v * cosine[...] + swapped * sine[...]).astype(jnp.bfloat16).astype(jnp.float32)

    rotated[...] = jnp.zeros_like(rotated)
    own_score[...] = jnp.zeros_like(own_score)
    own_value[...] = jnp.zeros_like(own_value)
    for kv in range(KVH):
        own_key = turn(head(HQ + kv))
        new_value = head(HQ + KVH + kv)
        for g in range(group):
            query = turn(head(kv * group + g))
            rotated[:, kv * PAD + g, :] = query
            score = jnp.sum(query * own_key, axis=1, keepdims=True) * inv_root
            own_score[:, kv * PAD + g, :] = jnp.broadcast_to(score, (seqs, HD))
            own_value[:, kv * PAD + g, :] = new_value

    @pl.loop(0, seqs)
    def _(s):
        place = lax.broadcasted_iota(jnp.int32, (1, positions), 1) + tp * positions
        is_live = place < lengths[s]
        for kv in range(KVH):
            at = slice(kv * HD, (kv + 1) * HD)
            lanes = slice(kv * PAD, (kv + 1) * PAD)
            query = rotated[s, lanes, :].astype(jnp.bfloat16)
            scores = lax.dot_general(
                query, k_held[s, :, at], (((1,), (1,)), ((), ())),
                preferred_element_type=jnp.float32,
            ) * inv_root
            scores = jnp.where(is_live, scores, jnp.float32(-1e30))
            top = jnp.max(scores, axis=1, keepdims=True)
            weights = jnp.where(is_live, jnp.exp(scores - top), 0.0).astype(jnp.bfloat16)
            total = jnp.sum(weights.astype(jnp.float32), axis=1, keepdims=True)
            parts[tp, 0, s, lanes, :] = jnp.dot(
                weights, v_held[s, :, at], preferred_element_type=jnp.float32
            )
            parts[tp, 1, s, lanes, :] = jnp.broadcast_to(top, (PAD, HD))
            parts[tp, 2, s, lanes, :] = jnp.broadcast_to(total, (PAD, HD))

    def send_parts(k):
        return remote(parts.at[tp], parts.at[tp], n_send.at[k], n_recv.at[k], peers[k - 1])

    for k in range(1, tps):
        send_parts(k).start()

    for d in range(2, planes - 1):
        relay(d)

    for k in range(1, tps):
        slot = parts.at[flip(tp, k, tps)]
        remote(slot, slot, n_send.at[k], n_recv.at[k], peers[k - 1]).wait_recv()

    @pl.loop(0, seqs)
    def _(s):
        mine = own_score[s]
        top = mine
        for t in range(tps):
            top = jnp.maximum(top, parts[t, 1, s])
        mine = jnp.exp(mine - top).astype(jnp.bfloat16).astype(jnp.float32)
        numerator, denominator = mine * own_value[s], mine
        for t in range(tps):
            scale = jnp.exp(parts[t, 1, s] - top)
            numerator = numerator + parts[t, 0, s] * scale
            denominator = denominator + parts[t, 2, s] * scale
        rotated[s] = numerator / denominator

    for j in range(HQ):
        row = (j // group) * PAD + j % group
        attended[:, j * HD : (j + 1) * HD] = rotated[:, row, :].astype(attended.dtype)

    @pl.loop(0, w_out.shape[1] // tile)
    def _(i):
        at = pl.ds(pl.multiple_of(i * tile, tile), tile)
        decoded[:, at] = jnp.dot(
            attended[...], w_out[:, at], preferred_element_type=jnp.float32
        ).astype(decoded.dtype)

    relay(planes - 1)

    for d in range(planes):
        for k in range(tps):
            for w in range(2):

                def from_twin(e):
                    target = rows_of(plane - e, 1 - core, k, w)
                    slot = e + planes - 1
                    return remote(
                        target, target, s_send.at[slot, k, w], s_recv.at[slot, k, w], twin
                    )

                @pl.when(plane >= d)
                def _():
                    from_twin(d).wait_recv()
                    to_twin(d, k, w).wait_send()

                    @pl.when(can_up)
                    def _():
                        to_up(d, k, w).wait_send()

                if d:

                    @pl.when(plane + d < planes)
                    def _():
                        from_twin(-d).wait_recv()
                        to_twin(-d, k, w).wait_send()

                @pl.when((plane + d < planes) & can_down)
                def _():
                    to_down(d, k, w).wait_send()

    for k in range(1, tps):
        for w in range(2):
            in_plane(k, w).wait_send()
        send_joined(k).wait_send()
        send_parts(k).wait_send()
    for copy in locals_:
        copy.wait()


def flush_kernel(decoded, qkv, out, decoded_to, qkv_to, out_to, sems):
    copies = [pltpu.make_async_copy(decoded, decoded_to, sems.at[0])]
    for source, target in ((qkv, qkv_to), (out, out_to)):
        rows = source.shape[0] // CUTS
        for i in range(CUTS):
            at = pl.ds(i * rows, rows)
            copies.append(
                pltpu.make_async_copy(source.at[at], target.at[at], sems.at[len(copies)])
            )
    for copy in copies:
        copy.start()
    for copy in copies:
        copy.wait()


def flush(*arrays):
    return pl.pallas_call(
        flush_kernel,
        out_shape=[jax.ShapeDtypeStruct(x.shape, x.dtype) for x in arrays],
        in_specs=[pl.BlockSpec(memory_space=pltpu.VMEM)] * 3,
        out_specs=[pl.BlockSpec(memory_space=pltpu.HBM)] * 3,
        scratch_shapes=[pltpu.SemaphoreType.DMA((2 * CUTS + 1,))],
        compiler_params=pltpu.CompilerParams(vmem_limit_bytes=2**20),
    )(*arrays)


def fused(mesh, hidden, lengths, old_qkv, old_out, keys, values, new_qkv, new_out):
    reps, tps = mesh.shape["rep"], mesh.shape["tp"]
    planes = reps // 2
    seqs = keys.shape[0]
    rows = new_qkv.shape[0]
    widths = (new_qkv.shape[1] // tps, new_out.shape[1] // tps)
    half = HD // 2
    frequency = ROPE_BASE ** (-2.0 * np.arange(half) / (2 * half))
    frequency = jnp.asarray(np.concatenate([frequency, frequency])[None], jnp.float32)

    sem = pltpu.SemaphoreType.DMA
    whole, anywhere = pl.BlockSpec(memory_space=pltpu.VMEM), pl.BlockSpec(memory_space=pl.ANY)
    in_hbm = pl.BlockSpec(memory_space=pltpu.HBM)
    f32, bf16 = jnp.float32, jnp.bfloat16
    padded = KVH * PAD
    landed = 2 * rows * reps * tps * sum(widths)
    scratch = [sem((tps, 2)), sem((tps, 2))]
    scratch += [sem((planes, tps, 2)) for _ in range(4)]
    scratch += [sem((2 * planes - 1, tps, 2)) for _ in range(2)]
    scratch += [sem((2,)), sem((4,))] + [sem((tps,)) for _ in range(4)]
    scratch += [pltpu.VMEM(x.shape, x.dtype) for x in (old_qkv, old_out, keys, values)]
    scratch += [
        pltpu.VMEM((tps, seqs, widths[0]), bf16),
        pltpu.VMEM((seqs, padded, HD), f32),
        pltpu.VMEM((seqs, padded, HD), f32),
        pltpu.VMEM((seqs, padded, HD), f32),
        pltpu.VMEM((tps, 3, seqs, padded, HD), f32),
        pltpu.VMEM((seqs, HQ * HD), bf16),
        pltpu.VMEM((seqs, HD), f32),
        pltpu.VMEM((seqs, HD), f32),
    ]
    return pl.pallas_call(
        functools.partial(step_kernel, planes, tps),
        out_shape=[pltpu.VMEM((seqs, widths[1]), bf16)]
        + [pltpu.VMEM((rows * reps * tps, width), bf16) for width in widths],
        in_specs=[whole, pl.BlockSpec(memory_space=pltpu.SMEM), whole] + [in_hbm] * 6,
        out_specs=[whole] + [anywhere] * 2,
        scratch_shapes=scratch,
        compiler_params=pltpu.CompilerParams(
            collective_id=0, has_side_effects=True, vmem_limit_bytes=VMEM_BYTES - landed - SLACK
        ),
    )(hidden, lengths, frequency, old_qkv, old_out, keys, values, new_qkv, new_out)


def solution(mesh):
    in_specs = (
        P("rep", None),
        P("rep"),
        P(None, "tp"),
        P(None, "tp"),
        P("rep", "tp", None),
        P("rep", "tp", None),
        P(("rep", "tp"), None),
        P(("rep", "tp"), None),
    )
    out_specs = (P("rep", "tp"), P(None, "tp"), P(None, "tp"))

    def step(*args):
        reps, tps = mesh.shape["rep"], mesh.shape["tp"]
        widths = [x.shape[1] // tps for x in args[6:]]
        tiled = args[6].shape[0] % 16 == 0 and all(width % 128 == 0 for width in widths)
        if reps % 4 or not tiled:
            return (per_device(*args[:6]), *native_move(*args[6:]))
        return tuple(flush(*fused(mesh, *args)))

    return jax.shard_map(
        step, mesh=mesh, in_specs=in_specs, out_specs=out_specs, check_vma=False
    )
```

profile of v0, /device:TPU:3, one launch (start us, length us, event | category | flops | bytes accessed | tf_op | source)
XLA Modules:
  0.0 132.8 jit_solution(16818114676861125894)
XLA Ops:
  0.6 126.8 %shard_map.112 = (bf16[4,896]{1,0:T(4,128)(2,1)S(1)}, bf16[3584,1152]{1,0:T(8,128)(2,1)S(1)}, bf16[3584,896]{1,0:T(8,128)(2,1)S(1)}) custom-call(bf16[4,3584]{1,0:T(4,128)(2,1)} %hidden.1, s32[4]{0:T(128)} %lengths.1, f32[1,128]{1,0:T(1,128)} %constant.2.clone.frequency, bf16[3584,1152]{1,0:T(8,128)(2,1)} %old_qkv.1, bf16[3584,896]{1,0:T(8,128)(2,1)} %old_out.1, ...), custom_call_target="tpu_custom_call" | custom-call | tf_op jit(solution)/shard_map/pallas_call | solution.py:469
  127.4 5.4 %shard_map.113 = (bf16[4,896]{1,0:T(4,128)(2,1)}, bf16[3584,1152]{1,0:T(8,128)(2,1)}, bf16[3584,896]{1,0:T(8,128)(2,1)}) custom-call(bf16[4,896]{1,0:T(4,128)(2,1)S(1)} %get-tuple-element.6.decoded, bf16[3584,1152]{1,0:T(8,128)(2,1)S(1)} %get-tuple-element.7.qkv, bf16[3584,896]{1,0:T(8,128)(2,1)S(1)} %get-tuple-element.8.out), custom_call_target="tpu_custom_call" | custom-call | tf_op jit(solution)/shard_map/pallas_call | solution.py:428
where the time goes:
time: 135 us; the launch traced here: 133 us
  Pallas kernels  132 us (98%)
    pallas_call x1, Pallas kernels, fused(): pl.pallas_call(functools.partial(step_kernel, planes, tps), out_shape=[pl...  127 us
    pallas_call x1, Pallas kernels, flush(): pl.pallas_call(flush_kernel, out_shape=[jax.ShapeDtypeStruct(x.shape, x.d...  5.36 us

commit v1 on v0

--- a/solution.py
+++ b/solution.py
@@ -13,6 +13,7 @@
 HD = 128
 PAD = 8
 CUTS = 8
+LAST = 3
 VMEM_BYTES = 67043328
 SLACK = 600000
 MESH = pl.DeviceIdType.MESH
@@ -109,12 +110,11 @@
 
 def step_kernel(
     planes, tps,
-    hidden, lengths, frequency, old_qkv, old_out, keys, values, new_qkv, new_out,
+    hidden_in, lengths_in, frequency_in, old_qkv, old_out, keys, values, new_qkv, new_out,
     decoded, qkv_full, out_full,
-    a_send, a_recv, u_send, u_recv, d_send, d_recv, s_send, s_recv, own_sem, load_sem,
-    j_send, j_recv, n_send, n_recv,
+    a_send, a_recv, z_send, z_recv, z_last, s_send, s_recv, s_last, own_sem, load_sem, small_sem,
     w_qkv, w_out, k_held, v_held, joined, rotated, own_score, own_value, parts, attended,
-    cosine, sine,
+    cosine, sine, hidden, frequency, lengths,
 ):
     rep, tp = lax.axis_index("rep"), lax.axis_index("tp")
     plane, core = rep // 2, rep % 2
@@ -125,10 +125,12 @@
     down = (jnp.maximum(plane - 1, 0) * 2 + core, tp)
     twin = (plane * 2 + 1 - core, tp)
     peers = [(rep, flip(tp, k, tps)) for k in range(1, tps)]
+    near = [k for k in range(1, tps) if k & (k - 1) == 0]
+    far = [k for k in range(1, tps) if k & (k - 1)]
     can_up, can_down = plane < planes - 1, plane > 0
 
     barrier = pltpu.get_barrier_semaphore()
-    for device in [twin] + peers:
+    for device in [twin] + [peers[k - 1] for k in near]:
         pl.semaphore_signal(barrier, inc=1, device_id=device, device_id_type=MESH)
 
     @pl.when(can_up)
@@ -139,13 +141,22 @@
     def _():
         pl.semaphore_signal(barrier, inc=1, device_id=down, device_id_type=MESH)
 
+    small = [
+        pltpu.make_async_copy(source, target, load_sem.at[4 + i])
+        for i, (source, target) in enumerate(
+            ((hidden_in, hidden), (frequency_in, frequency), (lengths_in, lengths))
+        )
+    ]
+    for copy in small:
+        copy.start()
+
     @pl.when(can_up & can_down)
     def _():
-        pl.semaphore_wait(barrier, tps + 2)
+        pl.semaphore_wait(barrier, len(near) + 3)
 
     @pl.when(jnp.logical_not(can_up & can_down))
     def _():
-        pl.semaphore_wait(barrier, tps + 1)
+        pl.semaphore_wait(barrier, len(near) + 2)
 
     def remote(source, target, send, recv, device):
         return pltpu.make_async_remote_copy(
@@ -153,84 +164,119 @@
             device_id=device, device_id_type=MESH,
         )
 
-    def rows_of(source_plane, source_core, k, w):
-        start = ((source_plane * 2 + source_core) * tps + flip(tp, k, tps)) * rows
-        return fulls[w].at[pl.ds(pl.multiple_of(start, rows), rows)]
+    def sent(ref, sem):
+        remote(ref, ref, sem, sem, twin).wait_send()
+
+    def landed(ref, sem):
+        remote(ref, ref, sem, sem, twin).wait_recv()
+
+    half = tps // 2
+
+    def at_rows(source_plane, source_core, first, count, w):
+        start = ((source_plane * 2 + source_core) * tps) * rows + first
+        return fulls[w].at[pl.ds(pl.multiple_of(start, 16), count)]
+
+    def piece_rows(source_plane, source_core, k, w):
+        return at_rows(source_plane, source_core, flip(tp, k, tps) * rows, rows, w)
+
+    def pair_first(h):
+        return (flip(tp, 2 * h, tps) // 2) * 2 * rows
+
+    def chunks(last):
+        cuts = [(h, w, 0, 2 * rows, None) for h in range(half) for w in range(2)]
+        if last:
+            h, w, _, count, _ = cuts.pop()
+            step = max(16, count // LAST // 16 * 16)
+            first = 0
+            for i in range(LAST):
+                size = step if i else count - (LAST - 1) * step
+                cuts.append((h, w, first, size, i))
+                first += size
+        return cuts
+
+    def chunk_rows(source_plane, source_core, chunk):
+        h, w, first, count, _ = chunk
+        return at_rows(source_plane, source_core, pair_first(h) + first, count, w)
+
+    def chunk_sem(sems, lasts, source_plane, chunk):
+        h, w, _, _, i = chunk
+        return sems.at[source_plane, h, w] if i is None else lasts.at[i]
+
+    def block_rows(source_plane, source_core, w):
+        return at_rows(source_plane, source_core, 0, tps * rows, w)
 
     def column(w, t):
         return blocks[w].at[:, pl.ds(pl.multiple_of(t * widths[w], 128), widths[w])]
 
     def in_plane(k, w):
-        return remote(
-            column(w, flip(tp, k, tps)), rows_of(plane, core, 0, w),
-            a_send.at[k, w], a_recv.at[k, w], peers[k - 1],
-        )
-
-    def piece(d, k, w):
-        target = rows_of(plane - d, core, k, w)
-        return target, (column(w, tp) if d == 0 and k == 0 else target)
-
-    def to_up(d, k, w):
-        target, source = piece(d, k, w)
-        return remote(source, target, u_send.at[d, k, w], u_recv.at[d, k, w], up)
-
-    def to_down(d, k, w):
-        target, source = piece(-d, k, w)
-        return remote(source, target, d_send.at[d, k, w], d_recv.at[d, k, w], down)
-
-    def to_twin(d, k, w):
-        target, source = piece(d, k, w)
-        slot = d + planes - 1
-        return remote(source, target, s_send.at[slot, k, w], s_recv.at[slot, k, w], twin)
+        remote(
+            column(w, flip(tp, k, tps)), piece_rows(plane, core, 0, w),
+            a_send.at[w], a_recv.at[k, w], peers[k - 1],
+        ).start()
 
     def own(k, w):
+        target = piece_rows(plane, core, k, w)
+        source = column(w, tp) if k == 0 else target
+        h = k // 2
+
         @pl.when(can_up)
         def _():
-            to_up(0, k, w).start()
+            remote(
+                source, target, z_send.at[plane, w], z_recv.at[plane, h, w], up
+            ).start()
 
         @pl.when(can_down)
         def _():
-            to_down(0, k, w).start()
-
-        to_twin(0, k, w).start()
+            remote(
+                source, target, z_send.at[plane + 1, w], z_recv.at[plane, h, w], down
+            ).start()
+
+        remote(source, target, s_send.at[plane, w], s_recv.at[plane, h, w], twin).start()
+
+    def take(source_plane, chunk, forward, slot, onward):
+        target = chunk_rows(source_plane, core, chunk)
+        landed(target, chunk_sem(z_recv, z_last, source_plane, chunk))
+        w = chunk[1]
+        if forward is not None:
+            can, device = forward
+
+            @pl.when(can)
+            def _():
+                for part in onward:
+                    ref = chunk_rows(source_plane, core, part)
+                    remote(
+                        ref, ref, z_send.at[slot, w],
+                        chunk_sem(z_recv, z_last, source_plane, part), device,
+                    ).start()
+
+        remote(
+            target, target, s_send.at[source_plane, w],
+            chunk_sem(s_recv, s_last, source_plane, chunk), twin,
+        ).start()
 
     def relay(d):
-        for k in range(tps):
-            for w in range(2):
-
-                @pl.when(plane >= d)
-                def _():
-                    target = rows_of(plane - d, core, k, w)
-                    remote(
-                        target, target, u_send.at[d - 1, k, w], u_recv.at[d - 1, k, w], up
-                    ).wait_recv()
-
-                    @pl.when(can_up)
-                    def _():
-                        to_up(d, k, w).start()
-
-                    to_twin(d, k, w).start()
-
-                @pl.when(plane + d < planes)
-                def _():
-                    target = rows_of(plane + d, core, k, w)
-                    remote(
-                        target, target, d_send.at[d - 1, k, w], d_recv.at[d - 1, k, w], down
-                    ).wait_recv()
-
-                    @pl.when(can_down)
-                    def _():
-                        to_down(d, k, w).start()
-
-                    to_twin(-d, k, w).start()
-
-    for k in range(1, tps):
-        for w in range(2):
-            in_plane(k, w).start()
+        cuts = chunks(d == planes - 1)
+        ahead = chunks(d == planes - 2)
+        for chunk in cuts:
+            onward = [part for part in ahead if part[:2] == chunk[:2]]
+            below = (can_up, up) if d < planes - 1 else None
+            above = (can_down, down) if d < planes - 1 else None
+
+            @pl.when(plane >= d)
+            def _():
+                take(plane - d, chunk, below, plane - d, onward)
+
+            @pl.when(plane + d < planes)
+            def _():
+                take(plane + d, chunk, above, plane + d + 1, onward)
+
     for w in range(2):
         own(0, w)
+    for k in near:
+        for w in range(2):
+            in_plane(k, w)
     locals_ = [
-        pltpu.make_async_copy(column(w, tp), rows_of(plane, core, 0, w), own_sem.at[w])
+        pltpu.make_async_copy(column(w, tp), piece_rows(plane, core, 0, w), own_sem.at[w])
         for w in range(2)
     ]
     loads = [
@@ -241,14 +287,17 @@
     ]
     for copy in locals_ + loads:
         copy.start()
-    for k in range(1, tps):
+    for k in near + far:
         for w in range(2):
-            target = rows_of(plane, core, k, w)
-            remote(
-                target, target, a_send.at[k, w], a_recv.at[k, w], peers[k - 1]
-            ).wait_recv()
+            landed(piece_rows(plane, core, k, w), a_recv.at[k, w])
             own(k, w)
-
+            if k == near[0] and w == 0:
+                for j in far:
+                    for v in range(2):
+                        in_plane(j, v)
+
+    for copy in small:
+        copy.wait()
     seqs = hidden.shape[0]
     lane = lax.broadcasted_iota(jnp.int32, (1, HD), 1)
     for s in range(seqs):
@@ -265,19 +314,15 @@
             hidden[...], w_qkv[:, at], preferred_element_type=jnp.float32
         ).astype(joined.dtype)
 
-    def send_joined(k):
-        return remote(
-            joined.at[tp], joined.at[tp], j_send.at[k], j_recv.at[k], peers[k - 1]
-        )
-
-    for k in range(1, tps):
-        send_joined(k).start()
+    def send_all(ref, send, recv):
+        for k in range(1, tps):
+            remote(ref.at[tp], ref.at[tp], send, recv, peers[k - 1]).start()
+
+    send_all(joined, small_sem.at[0], small_sem.at[1])
 
     relay(1)
 
-    for k in range(1, tps):
-        slot = joined.at[flip(tp, k, tps)]
-        remote(slot, slot, j_send.at[k], j_recv.at[k], peers[k - 1]).wait_recv()
+    landed(joined.at[pl.ds(0, tps - 1)], small_sem.at[1])
     for copy in loads[1:]:
         copy.wait()
 
@@ -329,18 +374,12 @@
             parts[tp, 1, s, lanes, :] = jnp.broadcast_to(top, (PAD, HD))
             parts[tp, 2, s, lanes, :] = jnp.broadcast_to(total, (PAD, HD))
 
-    def send_parts(k):
-        return remote(parts.at[tp], parts.at[tp], n_send.at[k], n_recv.at[k], peers[k - 1])
-
-    for k in range(1, tps):
-        send_parts(k).start()
+    send_all(parts, small_sem.at[2], small_sem.at[3])
 
     for d in range(2, planes - 1):
         relay(d)
 
-    for k in range(1, tps):
-        slot = parts.at[flip(tp, k, tps)]
-        remote(slot, slot, n_send.at[k], n_recv.at[k], peers[k - 1]).wait_recv()
+    landed(parts.at[pl.ds(0, tps - 1)], small_sem.at[3])
 
     @pl.loop(0, seqs)
     def _(s):
@@ -367,46 +406,64 @@
             attended[...], w_out[:, at], preferred_element_type=jnp.float32
         ).astype(decoded.dtype)
 
-    relay(planes - 1)
-
-    for d in range(planes):
-        for k in range(tps):
-            for w in range(2):
-
-                def from_twin(e):
-                    target = rows_of(plane - e, 1 - core, k, w)
-                    slot = e + planes - 1
-                    return remote(
-                        target, target, s_send.at[slot, k, w], s_recv.at[slot, k, w], twin
-                    )
-
-                @pl.when(plane >= d)
-                def _():
-                    from_twin(d).wait_recv()
-                    to_twin(d, k, w).wait_send()
-
-                    @pl.when(can_up)
-                    def _():
-                        to_up(d, k, w).wait_send()
-
-                if d:
-
-                    @pl.when(plane + d < planes)
-                    def _():
-                        from_twin(-d).wait_recv()
-                        to_twin(-d, k, w).wait_send()
-
-                @pl.when((plane + d < planes) & can_down)
-                def _():
-                    to_down(d, k, w).wait_send()
-
-    for k in range(1, tps):
+    def from_twin(source_plane, last):
+        for chunk in chunks(last):
+            landed(
+                chunk_rows(source_plane, 1 - core, chunk),
+                chunk_sem(s_recv, s_last, source_plane, chunk),
+            )
+
+    def to_twin(source_plane):
         for w in range(2):
-            in_plane(k, w).wait_send()
-        send_joined(k).wait_send()
-        send_parts(k).wait_send()
+            sent(block_rows(source_plane, core, w), s_send.at[source_plane, w])
+
+    def to_next(d):
+        for w in range(2):
+
+            @pl.when((plane >= d) & can_up)
+            def _():
+                sent(block_rows(plane - d, core, w), z_send.at[plane - d, w])
+
+            @pl.when((plane + d < planes) & can_down)
+            def _():
+                sent(block_rows(plane + d, core, w), z_send.at[plane + d + 1, w])
+
+    for w in range(2):
+        sent(fulls[w].at[pl.ds(0, (tps - 1) * rows)], a_send.at[w])
+    sent(joined.at[pl.ds(0, tps - 1)], small_sem.at[0])
+    sent(parts.at[pl.ds(0, tps - 1)], small_sem.at[2])
     for copy in locals_:
         copy.wait()
+    for d in range(planes - 1):
+
+        @pl.when(plane >= d)
+        def _():
+            from_twin(plane - d, False)
+            to_twin(plane - d)
+
+        if d:
+
+            @pl.when(plane + d < planes)
+            def _():
+                from_twin(plane + d, False)
+                to_twin(plane + d)
+
+    to_next(0)
+    relay(planes - 1)
+    d = planes - 1
+
+    @pl.when(plane >= d)
+    def _():
+        from_twin(plane - d, True)
+        to_twin(plane - d)
+
+    @pl.when(plane + d < planes)
+    def _():
+        from_twin(plane + d, True)
+        to_twin(plane + d)
+
+    for d in range(1, planes - 1):
+        to_next(d)
 
 
 def flush_kernel(decoded, qkv, out, decoded_to, qkv_to, out_to, sems):
@@ -451,10 +508,10 @@
     f32, bf16 = jnp.float32, jnp.bfloat16
     padded = KVH * PAD
     landed = 2 * rows * reps * tps * sum(widths)
-    scratch = [sem((tps, 2)), sem((tps, 2))]
-    scratch += [sem((planes, tps, 2)) for _ in range(4)]
-    scratch += [sem((2 * planes - 1, tps, 2)) for _ in range(2)]
-    scratch += [sem((2,)), sem((4,))] + [sem((tps,)) for _ in range(4)]
+    half = tps // 2
+    scratch = [sem((2,)), sem((tps, 2)), sem((planes + 1, 2)), sem((planes, half, 2)), sem((LAST,))]
+    scratch += [sem((planes, 2)), sem((planes, half, 2)), sem((LAST,))]
+    scratch += [sem((2,)), sem((7,)), sem((4,))]
     scratch += [pltpu.VMEM(x.shape, x.dtype) for x in (old_qkv, old_out, keys, values)]
     scratch += [
         pltpu.VMEM((tps, seqs, widths[0]), bf16),
@@ -465,12 +522,15 @@
         pltpu.VMEM((seqs, HQ * HD), bf16),
         pltpu.VMEM((seqs, HD), f32),
         pltpu.VMEM((seqs, HD), f32),
+        pltpu.VMEM(hidden.shape, hidden.dtype),
+        pltpu.VMEM(frequency.shape, frequency.dtype),
+        pltpu.SMEM(lengths.shape, lengths.dtype),
     ]
     return pl.pallas_call(
         functools.partial(step_kernel, planes, tps),
         out_shape=[pltpu.VMEM((seqs, widths[1]), bf16)]
         + [pltpu.VMEM((rows * reps * tps, width), bf16) for width in widths],
-        in_specs=[whole, pl.BlockSpec(memory_space=pltpu.SMEM), whole] + [in_hbm] * 6,
+        in_specs=[in_hbm] * 9,
         out_specs=[whole] + [anywhere] * 2,
         scratch_shapes=scratch,
         compiler_params=pltpu.CompilerParams(
@@ -496,7 +556,7 @@
         reps, tps = mesh.shape["rep"], mesh.shape["tp"]
         widths = [x.shape[1] // tps for x in args[6:]]
         tiled = args[6].shape[0] % 16 == 0 and all(width % 128 == 0 for width in widths)
-        if reps % 4 or not tiled:
+        if reps % 4 or reps < 6 or tps != 4 or not tiled:
             return (per_device(*args[:6]), *native_move(*args[6:]))
         return tuple(flush(*fused(mesh, *args)))
 

time: 135 us -> 131 us (0.970)
  Pallas kernels: 132 us -> 129 us
    pallas_call x1, Pallas kernels: 127 us -> 124 us  [fused(): pl.pallas_call(functools.partial(step_kernel, planes, tps), out_shape=[pl...]
where the time goes in v1:
time: 131 us; the launch traced here: 130 us
  Pallas kernels  129 us (98%)
    pallas_call x1, Pallas kernels, fused(): pl.pallas_call(functools.partial(step_kernel, planes, tps), out_shape=[pl...  124 us
    pallas_call x1, Pallas kernels, flush(): pl.pallas_call(flush_kernel, out_shape=[jax.ShapeDtypeStruct(x.shape, x.d...  5.36 us

profile of v1, /device:TPU:3, one launch (start us, length us, event | category | flops | bytes accessed | tf_op | source)
XLA Modules:
  0.0 130.1 jit_solution(8256393153583136860)
XLA Ops:
  0.6 124.1 %shard_map.112 = (bf16[4,896]{1,0:T(4,128)(2,1)S(1)}, bf16[3584,1152]{1,0:T(8,128)(2,1)S(1)}, bf16[3584,896]{1,0:T(8,128)(2,1)S(1)}) custom-call(bf16[4,3584]{1,0:T(4,128)(2,1)} %hidden_in.1, s32[4]{0:T(128)} %lengths_in.1, f32[1,128]{1,0:T(1,128)} %constant.2.clone.frequency_in, bf16[3584,1152]{1,0:T(8,128)(2,1)} %old_qkv.1, bf16[3584,896]{1,0:T(8,128)(2,1)} %old_out.1, ...), custom_call_target="tpu_custom_call" | custom-call | tf_op jit(solution)/shard_map/pallas_call | solution.py:529
  124.7 5.4 %shard_map.113 = (bf16[4,896]{1,0:T(4,128)(2,1)}, bf16[3584,1152]{1,0:T(8,128)(2,1)}, bf16[3584,896]{1,0:T(8,128)(2,1)}) custom-call(bf16[4,896]{1,0:T(4,128)(2,1)S(1)} %get-tuple-element.6.decoded, bf16[3584,1152]{1,0:T(8,128)(2,1)S(1)} %get-tuple-element.7.qkv, bf16[3584,896]{1,0:T(8,128)(2,1)S(1)} %get-tuple-element.8.out), custom_call_target="tpu_custom_call" | custom-call | tf_op jit(solution)/shard_map/pallas_call | solution.py:485

commit v2 on v1

--- a/solution.py
+++ b/solution.py
@@ -12,8 +12,8 @@
 KVH = 4
 HD = 128
 PAD = 8
-CUTS = 8
-LAST = 3
+CUTS = 28
+TAIL = 4
 VMEM_BYTES = 67043328
 SLACK = 600000
 MESH = pl.DeviceIdType.MESH
@@ -112,15 +112,18 @@
     planes, tps,
     hidden_in, lengths_in, frequency_in, old_qkv, old_out, keys, values, new_qkv, new_out,
     decoded, qkv_full, out_full,
-    a_send, a_recv, z_send, z_recv, z_last, s_send, s_recv, s_last, own_sem, load_sem, small_sem,
+    a_send, a_recv, z_send, z_recv, z_last, s_send, s_recv, t_send, t_recv, own_sem,
+    load_sem, small_sem, met,
+    stage,
     w_qkv, w_out, k_held, v_held, joined, rotated, own_score, own_value, parts, attended,
     cosine, sine, hidden, frequency, lengths,
 ):
     rep, tp = lax.axis_index("rep"), lax.axis_index("tp")
     plane, core = rep // 2, rep % 2
     rows = new_qkv.shape[0]
-    blocks, fulls = (new_qkv, new_out), (qkv_full, out_full)
+    fulls = (qkv_full, out_full)
     widths = (qkv_full.shape[1], out_full.shape[1])
+    bases = (0, new_qkv.shape[1])
     up = (jnp.minimum(plane + 1, planes - 1) * 2 + core, tp)
     down = (jnp.maximum(plane - 1, 0) * 2 + core, tp)
     twin = (plane * 2 + 1 - core, tp)
@@ -130,33 +133,66 @@
     can_up, can_down = plane < planes - 1, plane > 0
 
     barrier = pltpu.get_barrier_semaphore()
-    for device in [twin] + [peers[k - 1] for k in near]:
-        pl.semaphore_signal(barrier, inc=1, device_id=device, device_id_type=MESH)
+    beside = [twin] + [peers[k - 1] for k in near]
+
+    def tell(semaphore, device):
+        pl.semaphore_signal(semaphore, inc=1, device_id=device, device_id_type=MESH)
 
     @pl.when(can_up)
     def _():
-        pl.semaphore_signal(barrier, inc=1, device_id=up, device_id_type=MESH)
-
-    @pl.when(can_down)
-    def _():
-        pl.semaphore_signal(barrier, inc=1, device_id=down, device_id_type=MESH)
-
+        tell(barrier, up)
+
+    @pl.when(can_down & (plane != 2))
+    def _():
+        tell(barrier, down)
+
+    @pl.when(plane != 1)
+    def _():
+        for device in beside:
+            tell(barrier, device)
+
+    half = tps // 2
+
+    def at_rows(source_plane, source_core, first, count, w):
+        start = ((source_plane * 2 + source_core) * tps) * rows + first
+        return fulls[w].at[pl.ds(pl.multiple_of(start, 16), count)]
+
+    def piece_rows(source_plane, source_core, k, w):
+        return at_rows(source_plane, source_core, flip(tp, k, tps) * rows, rows, w)
+
+    mine = [
+        pltpu.make_async_copy(
+            source.at[:, pl.ds(pl.multiple_of(tp * widths[w], 128), widths[w])],
+            piece_rows(plane, core, 0, w), own_sem.at[w],
+        )
+        for w, source in enumerate((new_qkv, new_out))
+    ]
+    staged = [
+        pltpu.make_async_copy(
+            source, stage.at[:, pl.ds(bases[w], source.shape[1])], own_sem.at[2 + w]
+        )
+        for w, source in enumerate((new_qkv, new_out))
+    ]
+    for copy in mine + staged:
+        copy.start()
     small = [
         pltpu.make_async_copy(source, target, load_sem.at[4 + i])
         for i, (source, target) in enumerate(
             ((hidden_in, hidden), (frequency_in, frequency), (lengths_in, lengths))
         )
     ]
-    for copy in small:
-        copy.start()
-
-    @pl.when(can_up & can_down)
-    def _():
-        pl.semaphore_wait(barrier, len(near) + 3)
+
+    @pl.when(plane == 1)
+    def _():
+        pl.semaphore_wait(barrier, 1)
+
+    @pl.when((plane != 1) & can_up & can_down)
+    def _():
+        pl.semaphore_wait(barrier, len(beside) + 2)
 
     @pl.when(jnp.logical_not(can_up & can_down))
     def _():
-        pl.semaphore_wait(barrier, len(near) + 2)
+        pl.semaphore_wait(barrier, len(beside) + 1)
 
     def remote(source, target, send, recv, device):
         return pltpu.make_async_remote_copy(
@@ -170,131 +206,197 @@
     def landed(ref, sem):
         remote(ref, ref, sem, sem, twin).wait_recv()
 
-    half = tps // 2
-
-    def at_rows(source_plane, source_core, first, count, w):
-        start = ((source_plane * 2 + source_core) * tps) * rows + first
-        return fulls[w].at[pl.ds(pl.multiple_of(start, 16), count)]
-
-    def piece_rows(source_plane, source_core, k, w):
-        return at_rows(source_plane, source_core, flip(tp, k, tps) * rows, rows, w)
-
     def pair_first(h):
         return (flip(tp, 2 * h, tps) // 2) * 2 * rows
 
-    def chunks(last):
-        cuts = [(h, w, 0, 2 * rows, None) for h in range(half) for w in range(2)]
+    tail = TAIL * 16
+    tails = [(1, first, count) for first, count in ((2 * rows - tail, tail - 16), (2 * rows - 16, 16))]
+    tails = [(c, part) for part in tails for c in (1, 0)]
+
+    def parts_of(h, last):
+        if last and h == half - 1:
+            return [(0, 0, 2 * rows, 0), (1, 0, 2 * rows - tail, 1)]
+        return [(w, 0, 2 * rows, None) for w in range(2)]
+
+    def part_rows(source_plane, source_core, h, part):
+        w, first, count = part[:3]
+        return at_rows(source_plane, source_core, pair_first(h) + first, count, w)
+
+    def part_sem(source_plane, h, part):
+        return z_recv.at[source_plane, h] if part[3] is None else z_last.at[part[3]]
+
+    def bytes_of(parts):
+        return stage.at[:, pl.ds(0, stage.shape[1] // tps * parts)]
+
+    def out_rows(count):
+        return out_full.at[pl.ds(0, count)]
+
+    def block_bytes(last):
         if last:
-            h, w, _, count, _ = cuts.pop()
-            step = max(16, count // LAST // 16 * 16)
-            first = 0
-            for i in range(LAST):
-                size = step if i else count - (LAST - 1) * step
-                cuts.append((h, w, first, size, i))
-                first += size
-        return cuts
-
-    def chunk_rows(source_plane, source_core, chunk):
-        h, w, first, count, _ = chunk
-        return at_rows(source_plane, source_core, pair_first(h) + first, count, w)
-
-    def chunk_sem(sems, lasts, source_plane, chunk):
-        h, w, _, _, i = chunk
-        return sems.at[source_plane, h, w] if i is None else lasts.at[i]
-
-    def block_rows(source_plane, source_core, w):
-        return at_rows(source_plane, source_core, 0, tps * rows, w)
+            return out_rows(rows * tps * sum(widths) // widths[1] - tail)
+        return stage
+
+    def send_tails(source_plane, device):
+        for i, (c, part) in enumerate(tails):
+            ref = part_rows(source_plane, c, half - 1, part)
+            remote(ref, ref, t_send.at[0], t_recv.at[i], device).start()
+
+    def take_tails(source_plane):
+        for i, (c, part) in enumerate(tails):
+            ref = part_rows(source_plane, c, half - 1, part)
+            landed(ref, t_recv.at[i])
+            remote(ref, ref, t_send.at[1], t_recv.at[len(tails)], twin).start()
 
     def column(w, t):
-        return blocks[w].at[:, pl.ds(pl.multiple_of(t * widths[w], 128), widths[w])]
+        start = bases[w] + t * widths[w]
+        return stage.at[:, pl.ds(pl.multiple_of(start, 128), widths[w])]
 
     def in_plane(k, w):
         remote(
             column(w, flip(tp, k, tps)), piece_rows(plane, core, 0, w),
-            a_send.at[w], a_recv.at[k, w], peers[k - 1],
+            a_send.at[0], a_recv.at[k - 1, w], peers[k - 1],
         ).start()
 
-    def own(k, w):
-        target = piece_rows(plane, core, k, w)
-        source = column(w, tp) if k == 0 else target
-        h = k // 2
+    def own_up(k, w):
+        ref = piece_rows(plane, core, k, w)
 
         @pl.when(can_up)
         def _():
-            remote(
-                source, target, z_send.at[plane, w], z_recv.at[plane, h, w], up
-            ).start()
+            remote(ref, ref, z_send.at[plane], z_recv.at[plane, k // 2], up).start()
+
+    def own_down(k, w):
+        ref = piece_rows(plane, core, k, w)
 
         @pl.when(can_down)
         def _():
-            remote(
-                source, target, z_send.at[plane + 1, w], z_recv.at[plane, h, w], down
-            ).start()
-
-        remote(source, target, s_send.at[plane, w], s_recv.at[plane, h, w], twin).start()
-
-    def take(source_plane, chunk, forward, slot, onward):
-        target = chunk_rows(source_plane, core, chunk)
-        landed(target, chunk_sem(z_recv, z_last, source_plane, chunk))
-        w = chunk[1]
+            remote(ref, ref, z_send.at[plane + 1], z_recv.at[plane, k // 2], down).start()
+
+    def own_twin(k, w):
+        ref = piece_rows(plane, core, k, w)
+        remote(ref, ref, s_send.at[plane], s_recv.at[plane], twin).start()
+
+    def take(source_plane, h, last, parts, forward, slot, onward):
+        if last:
+            (part,) = parts
+            landed(part_rows(source_plane, core, h, part), part_sem(source_plane, h, part))
+        else:
+            landed(bytes_of(2), z_recv.at[source_plane, h])
         if forward is not None:
             can, device = forward
 
             @pl.when(can)
             def _():
                 for part in onward:
-                    ref = chunk_rows(source_plane, core, part)
+                    ref = part_rows(source_plane, core, h, part)
                     remote(
-                        ref, ref, z_send.at[slot, w],
-                        chunk_sem(z_recv, z_last, source_plane, part), device,
+                        ref, ref, z_send.at[slot], part_sem(source_plane, h, part), device
                     ).start()
 
-        remote(
-            target, target, s_send.at[source_plane, w],
-            chunk_sem(s_recv, s_last, source_plane, chunk), twin,
-        ).start()
+        for part in parts:
+            ref = part_rows(source_plane, core, h, part)
+            remote(ref, ref, s_send.at[source_plane], s_recv.at[source_plane], twin).start()
 
     def relay(d):
-        cuts = chunks(d == planes - 1)
-        ahead = chunks(d == planes - 2)
-        for chunk in cuts:
-            onward = [part for part in ahead if part[:2] == chunk[:2]]
-            below = (can_up, up) if d < planes - 1 else None
-            above = (can_down, down) if d < planes - 1 else None
-
-            @pl.when(plane >= d)
-            def _():
-                take(plane - d, chunk, below, plane - d, onward)
+        ends = d == planes - 1
+        for h in range(half):
+            cuts = parts_of(h, ends)
+            onward = parts_of(h, d == planes - 2)
+            single = ends and h == half - 1
+            for parts in [[part] for part in cuts] if single else [cuts]:
+
+                @pl.when(plane >= d)
+                def _():
+                    take(plane - d, h, single, parts, None if ends else (can_up, up), plane - d, onward)
+
+                @pl.when(plane + d < planes)
+                def _():
+                    take(
+                        plane + d, h, single, parts,
+                        None if ends else (can_down, down), plane + d + 1, onward,
+                    )
+
+    def settle_twin(source_plane, last):
+        landed(block_bytes(last), s_recv.at[source_plane])
+        sent(block_bytes(last), s_send.at[source_plane])
+
+    def settle_next(d):
+        @pl.when((plane >= d) & can_up)
+        def _():
+            sent(block_bytes(d == planes - 2), z_send.at[plane - d])
+
+        @pl.when((plane + d < planes) & can_down)
+        def _():
+            sent(block_bytes(d == planes - 2), z_send.at[plane + d + 1])
+
+    def settle(d):
+        @pl.when(plane >= d)
+        def _():
+            settle_twin(plane - d, d == planes - 1)
+
+        if d:
 
             @pl.when(plane + d < planes)
             def _():
-                take(plane + d, chunk, above, plane + d + 1, onward)
+                settle_twin(plane + d, d == planes - 1)
 
     for w in range(2):
-        own(0, w)
-    for k in near:
+        mine[w].wait()
+        own_down(0, w)
+
+    def open_plane():
+        for w in (1, 0):
+            staged[w].wait()
+            for k in near:
+                in_plane(k, w)
         for w in range(2):
-            in_plane(k, w)
-    locals_ = [
-        pltpu.make_async_copy(column(w, tp), piece_rows(plane, core, 0, w), own_sem.at[w])
-        for w in range(2)
-    ]
+            own_twin(0, w)
+
+    @pl.when(plane == 0)
+    def _():
+        for device in beside:
+            tell(met.at[0], device)
+
+    @pl.when(plane == 2)
+    def _():
+        tell(met.at[1], down)
+
+    @pl.when(plane != 1)
+    def _():
+        for w in range(2):
+            own_up(0, w)
+        open_plane()
+
+    @pl.when(plane == 0)
+    def _():
+        pl.semaphore_wait(met.at[0], len(beside))
+        tell(met.at[2], up)
+
+    @pl.when(plane == 1)
+    def _():
+        pl.semaphore_wait(met.at[2], 1)
+        open_plane()
+        pl.semaphore_wait(met.at[1], 1)
+        for w in range(2):
+            own_up(0, w)
+
     loads = [
         pltpu.make_async_copy(source, target, load_sem.at[i])
         for i, (source, target) in enumerate(
             ((old_qkv, w_qkv), (keys, k_held), (values, v_held), (old_out, w_out))
         )
     ]
-    for copy in locals_ + loads:
+    for copy in loads + small:
         copy.start()
-    for k in near + far:
-        for w in range(2):
-            landed(piece_rows(plane, core, k, w), a_recv.at[k, w])
-            own(k, w)
-            if k == near[0] and w == 0:
-                for j in far:
-                    for v in range(2):
-                        in_plane(j, v)
+    arrivals = [(k, w) for w in (1, 0) for k in near] + [(k, w) for k in far for w in (1, 0)]
+    for k, w in arrivals:
+        landed(piece_rows(plane, core, k, w), a_recv.at[k - 1, w])
+        own_down(k, w)
+        own_up(k, w)
+        own_twin(k, w)
+        if (k, w) == arrivals[0]:
+            for j in far:
+                for v in (1, 0):
+                    in_plane(j, v)
 
     for copy in small:
         copy.wait()
@@ -378,6 +480,16 @@
 
     for d in range(2, planes - 1):
         relay(d)
+    settle(planes - 2)
+
+    @pl.when((core == 1) & (plane == planes - 2))
+    def _():
+        send_tails(0, up)
+
+    @pl.when((core == 1) & (plane == 1))
+    def _():
+        send_tails(planes - 1, down)
+
 
     landed(parts.at[pl.ds(0, tps - 1)], small_sem.at[3])
 
@@ -406,79 +518,51 @@
             attended[...], w_out[:, at], preferred_element_type=jnp.float32
         ).astype(decoded.dtype)
 
-    def from_twin(source_plane, last):
-        for chunk in chunks(last):
-            landed(
-                chunk_rows(source_plane, 1 - core, chunk),
-                chunk_sem(s_recv, s_last, source_plane, chunk),
-            )
-
-    def to_twin(source_plane):
-        for w in range(2):
-            sent(block_rows(source_plane, core, w), s_send.at[source_plane, w])
-
-    def to_next(d):
-        for w in range(2):
-
-            @pl.when((plane >= d) & can_up)
-            def _():
-                sent(block_rows(plane - d, core, w), z_send.at[plane - d, w])
-
-            @pl.when((plane + d < planes) & can_down)
-            def _():
-                sent(block_rows(plane + d, core, w), z_send.at[plane + d + 1, w])
-
-    for w in range(2):
-        sent(fulls[w].at[pl.ds(0, (tps - 1) * rows)], a_send.at[w])
+    sent(bytes_of(tps - 1), a_send.at[0])
     sent(joined.at[pl.ds(0, tps - 1)], small_sem.at[0])
     sent(parts.at[pl.ds(0, tps - 1)], small_sem.at[2])
-    for copy in locals_:
-        copy.wait()
-    for d in range(planes - 1):
-
-        @pl.when(plane >= d)
-        def _():
-            from_twin(plane - d, False)
-            to_twin(plane - d)
-
-        if d:
-
-            @pl.when(plane + d < planes)
-            def _():
-                from_twin(plane + d, False)
-                to_twin(plane + d)
-
-    to_next(0)
+    for d in range(planes - 2):
+        settle(d)
+    settle_next(0)
     relay(planes - 1)
-    d = planes - 1
-
-    @pl.when(plane >= d)
-    def _():
-        from_twin(plane - d, True)
-        to_twin(plane - d)
-
-    @pl.when(plane + d < planes)
-    def _():
-        from_twin(plane + d, True)
-        to_twin(plane + d)
+
+    @pl.when((core == 1) & (plane == planes - 1))
+    def _():
+        take_tails(0)
+
+    @pl.when((core == 1) & (plane == 0))
+    def _():
+        take_tails(planes - 1)
+
+    settle(planes - 1)
+    at_end = (plane == 0) | (plane == planes - 1)
+
+    @pl.when(at_end & (core == 1))
+    def _():
+        sent(out_rows(2 * tail), t_send.at[1])
+
+    @pl.when(at_end & (core == 0))
+    def _():
+        landed(out_rows(2 * tail), t_recv.at[len(tails)])
 
     for d in range(1, planes - 1):
-        to_next(d)
+        settle_next(d)
+
+    @pl.when((core == 1) & ((plane == 1) | (plane == planes - 2)))
+    def _():
+        sent(out_rows(2 * tail), t_send.at[0])
 
 
 def flush_kernel(decoded, qkv, out, decoded_to, qkv_to, out_to, sems):
-    copies = [pltpu.make_async_copy(decoded, decoded_to, sems.at[0])]
-    for source, target in ((qkv, qkv_to), (out, out_to)):
-        rows = source.shape[0] // CUTS
-        for i in range(CUTS):
-            at = pl.ds(i * rows, rows)
-            copies.append(
-                pltpu.make_async_copy(source.at[at], target.at[at], sems.at[len(copies)])
-            )
-    for copy in copies:
-        copy.start()
-    for copy in copies:
-        copy.wait()
+    pairs = ((decoded, decoded_to), (qkv, qkv_to), (out, out_to))
+    for i, (source, target) in enumerate(pairs):
+        cuts = max(c for c in range(1, CUTS + 1) if c == 1 or source.shape[0] % (16 * c) == 0)
+        rows = source.shape[0] // cuts
+        for j in range(cuts):
+            at = pl.ds(j * rows, rows)
+            pltpu.make_async_copy(source.at[at], target.at[at], sems.at[i]).start()
+    for i, (source, target) in enumerate(pairs):
+        pltpu.make_async_copy(source, target, sems.at[i]).wait()
 
 
 def flush(*arrays):
@@ -487,7 +571,7 @@
         out_shape=[jax.ShapeDtypeStruct(x.shape, x.dtype) for x in arrays],
         in_specs=[pl.BlockSpec(memory_space=pltpu.VMEM)] * 3,
         out_specs=[pl.BlockSpec(memory_space=pltpu.HBM)] * 3,
-        scratch_shapes=[pltpu.SemaphoreType.DMA((2 * CUTS + 1,))],
+        scratch_shapes=[pltpu.SemaphoreType.DMA((3,))],
         compiler_params=pltpu.CompilerParams(vmem_limit_bytes=2**20),
     )(*arrays)
 
@@ -508,10 +592,10 @@
     f32, bf16 = jnp.float32, jnp.bfloat16
     padded = KVH * PAD
     landed = 2 * rows * reps * tps * sum(widths)
-    half = tps // 2
-    scratch = [sem((2,)), sem((tps, 2)), sem((planes + 1, 2)), sem((planes, half, 2)), sem((LAST,))]
-    scratch += [sem((planes, 2)), sem((planes, half, 2)), sem((LAST,))]
-    scratch += [sem((2,)), sem((7,)), sem((4,))]
+    scratch = [sem((1,)), sem((tps - 1, 2)), sem((planes + 1,)), sem((planes, tps // 2)), sem((2,))]
+    scratch += [sem((planes,)), sem((planes,)), sem((2,)), sem((5,))]
+    scratch += [sem((4,)), sem((7,)), sem((4,)), pltpu.SemaphoreType.REGULAR((3,))]
+    scratch += [pltpu.VMEM((rows, new_qkv.shape[1] + new_out.shape[1]), bf16)]
     scratch += [pltpu.VMEM(x.shape, x.dtype) for x in (old_qkv, old_out, keys, values)]
     scratch += [
         pltpu.VMEM((tps, seqs, widths[0]), bf16),
@@ -555,7 +639,9 @@
     def step(*args):
         reps, tps = mesh.shape["rep"], mesh.shape["tp"]
         widths = [x.shape[1] // tps for x in args[6:]]
-        tiled = args[6].shape[0] % 16 == 0 and all(width % 128 == 0 for width in widths)
+        rows = args[6].shape[0]
+        tiled = rows % 16 == 0 and all(width % 128 == 0 for width in widths)
+        tiled = tiled and rows > TAIL * 8 and rows * tps * sum(widths) % widths[1] == 0
         if reps % 4 or reps < 6 or tps != 4 or not tiled:
             return (per_device(*args[:6]), *native_move(*args[6:]))
         return tuple(flush(*fused(mesh, *args)))

time: 131 us -> 130 us (level)
    pallas_call x1, Pallas kernels: 124 us -> 123 us  [fused(): pl.pallas_call(functools.partial(step_kernel, planes, tps), out_shape=[pl...]
where the time goes in v2:
time: 130 us; the launch traced here: 128 us
  Pallas kernels  128 us (98%)
    pallas_call x1, Pallas kernels, fused(): pl.pallas_call(functools.partial(step_kernel, planes, tps), out_shape=[pl...  123 us
    pallas_call x1, Pallas kernels, flush(): pl.pallas_call(flush_kernel, out_shape=[jax.ShapeDtypeStruct(x.shape, x.d...  5.18 us

profile of v2, /device:TPU:3, one launch (start us, length us, event | category | flops | bytes accessed | tf_op | source)
XLA Modules:
  0.0 128.4 jit_solution(9221297934763888809)
XLA Ops:
  0.6 122.6 %shard_map.112 = (bf16[4,896]{1,0:T(4,128)(2,1)S(1)}, bf16[3584,1152]{1,0:T(8,128)(2,1)S(1)}, bf16[3584,896]{1,0:T(8,128)(2,1)S(1)}) custom-call(bf16[4,3584]{1,0:T(4,128)(2,1)} %hidden_in.1, s32[4]{0:T(128)} %lengths_in.1, f32[1,128]{1,0:T(1,128)} %constant.2.clone.frequency_in, bf16[3584,1152]{1,0:T(8,128)(2,1)} %old_qkv.1, bf16[3584,896]{1,0:T(8,128)(2,1)} %old_out.1, ...), custom_call_target="tpu_custom_call" | custom-call | tf_op jit(solution)/shard_map/pallas_call | solution.py:613
  123.2 5.2 %shard_map.113 = (bf16[4,896]{1,0:T(4,128)(2,1)}, bf16[3584,1152]{1,0:T(8,128)(2,1)}, bf16[3584,896]{1,0:T(8,128)(2,1)}) custom-call(bf16[4,896]{1,0:T(4,128)(2,1)S(1)} %get-tuple-element.6.decoded, bf16[3584,1152]{1,0:T(8,128)(2,1)S(1)} %get-tuple-element.7.qkv, bf16[3584,896]{1,0:T(8,128)(2,1)S(1)} %get-tuple-element.8.out), custom_call_target="tpu_custom_call" | custom-call | tf_op jit(solution)/shard_map/pallas_call | solution.py:569

commit v3 on v2

--- a/solution.py
+++ b/solution.py
@@ -14,6 +14,7 @@
 PAD = 8
 CUTS = 28
 TAIL = 4
+DETOUR = 16
 VMEM_BYTES = 67043328
 SLACK = 600000
 MESH = pl.DeviceIdType.MESH
@@ -113,8 +114,8 @@
     hidden_in, lengths_in, frequency_in, old_qkv, old_out, keys, values, new_qkv, new_out,
     decoded, qkv_full, out_full,
     a_send, a_recv, z_send, z_recv, z_last, s_send, s_recv, t_send, t_recv, own_sem,
-    load_sem, small_sem, met,
-    stage,
+    load_sem, small_sem, met, d_send, d_recv,
+    stage, detour,
     w_qkv, w_out, k_held, v_held, joined, rotated, own_score, own_value, parts, attended,
     cosine, sine, hidden, frequency, lengths,
 ):
@@ -132,25 +133,6 @@
     far = [k for k in range(1, tps) if k & (k - 1)]
     can_up, can_down = plane < planes - 1, plane > 0
 
-    barrier = pltpu.get_barrier_semaphore()
-    beside = [twin] + [peers[k - 1] for k in near]
-
-    def tell(semaphore, device):
-        pl.semaphore_signal(semaphore, inc=1, device_id=device, device_id_type=MESH)
-
-    @pl.when(can_up)
-    def _():
-        tell(barrier, up)
-
-    @pl.when(can_down & (plane != 2))
-    def _():
-        tell(barrier, down)
-
-    @pl.when(plane != 1)
-    def _():
-        for device in beside:
-            tell(barrier, device)
-
     half = tps // 2
 
     def at_rows(source_plane, source_core, first, count, w):
@@ -175,6 +157,25 @@
     ]
     for copy in mine + staged:
         copy.start()
+    barrier = pltpu.get_barrier_semaphore()
+    beside = [twin] + [peers[k - 1] for k in near]
+
+    def tell(semaphore, device):
+        pl.semaphore_signal(semaphore, inc=1, device_id=device, device_id_type=MESH)
+
+    @pl.when(can_up)
+    def _():
+        tell(barrier, up)
+
+    @pl.when(can_down & (plane != 2))
+    def _():
+        tell(barrier, down)
+
+    @pl.when(plane != 1)
+    def _():
+        for device in beside:
+            tell(barrier, device)
+
     small = [
         pltpu.make_async_copy(source, target, load_sem.at[4 + i])
         for i, (source, target) in enumerate(
@@ -267,13 +268,45 @@
     def own_down(k, w):
         ref = piece_rows(plane, core, k, w)
 
-        @pl.when(can_down)
-        def _():
+        def send(ref):
             remote(ref, ref, z_send.at[plane + 1], z_recv.at[plane, k // 2], down).start()
+
+        if w and k:
+            short = detoured & (core == (k + 1) % 2)
+
+            @pl.when(short)
+            def _():
+                send(at_rows(plane, core, flip(tp, k, tps) * rows, rows - DETOUR, w))
+
+            @pl.when(can_down & jnp.logical_not(short))
+            def _():
+                send(ref)
+
+        else:
+
+            @pl.when(can_down)
+            def _():
+                send(ref)
 
     def own_twin(k, w):
         ref = piece_rows(plane, core, k, w)
         remote(ref, ref, s_send.at[plane], s_recv.at[plane], twin).start()
+
+    detoured = (plane == 1) & (tp == 0)
+    carries = (tp != 0) & (core == (tp + 1) % 2)
+
+    def detour_down():
+        @pl.when((plane == 1) & carries)
+        def _():
+            source = stage.at[pl.ds(rows - DETOUR, DETOUR), pl.ds(bases[1], widths[1])]
+            remote(source, detour, d_send.at[0], d_recv.at[0], down).start()
+
+    def detour_across():
+        @pl.when((plane == 0) & carries)
+        def _():
+            landed(detour, d_recv.at[0])
+            target = at_rows(1, core, tp * rows + rows - DETOUR, DETOUR, 1)
+            remote(detour, target, d_send.at[0], z_recv.at[1, tp // 2], (rep, jnp.int32(0))).start()
 
     def take(source_plane, h, last, parts, forward, slot, onward):
         if last:
@@ -319,6 +352,30 @@
         landed(block_bytes(last), s_recv.at[source_plane])
         sent(block_bytes(last), s_send.at[source_plane])
 
+    def settle_own():
+        cut = rows * tps * sum(widths) // widths[1]
+        shorts = [
+            (c, cut - DETOUR * sum((k + 1) % 2 == c for k in range(1, tps))) for c in range(2)
+        ]
+
+        @pl.when(can_up)
+        def _():
+            sent(stage, z_send.at[plane])
+
+        @pl.when(can_down & jnp.logical_not(detoured))
+        def _():
+            sent(stage, z_send.at[plane + 1])
+
+        for c, count in shorts:
+
+            @pl.when(detoured & (core == c))
+            def _():
+                sent(out_rows(count), z_send.at[plane + 1])
+
+        @pl.when((plane < 2) & carries)
+        def _():
+            sent(detour, d_send.at[0])
+
     def settle_next(d):
         @pl.when((plane >= d) & can_up)
         def _():
@@ -375,6 +432,7 @@
     def _():
         pl.semaphore_wait(met.at[2], 1)
         open_plane()
+        detour_down()
         pl.semaphore_wait(met.at[1], 1)
         for w in range(2):
             own_up(0, w)
@@ -398,6 +456,7 @@
                 for v in (1, 0):
                     in_plane(j, v)
 
+    detour_across()
     for copy in small:
         copy.wait()
     seqs = hidden.shape[0]
@@ -523,7 +582,7 @@
     sent(parts.at[pl.ds(0, tps - 1)], small_sem.at[2])
     for d in range(planes - 2):
         settle(d)
-    settle_next(0)
+    settle_own()
     relay(planes - 1)
 
     @pl.when((core == 1) & (plane == planes - 1))
@@ -595,7 +654,9 @@
     scratch = [sem((1,)), sem((tps - 1, 2)), sem((planes + 1,)), sem((planes, tps // 2)), sem((2,))]
     scratch += [sem((planes,)), sem((planes,)), sem((2,)), sem((5,))]
     scratch += [sem((4,)), sem((7,)), sem((4,)), pltpu.SemaphoreType.REGULAR((3,))]
+    scratch += [sem((1,)), sem((1,))]
     scratch += [pltpu.VMEM((rows, new_qkv.shape[1] + new_out.shape[1]), bf16)]
+    scratch += [pltpu.VMEM((DETOUR, widths[1]), bf16)]
     scratch += [pltpu.VMEM(x.shape, x.dtype) for x in (old_qkv, old_out, keys, values)]
     scratch += [
         pltpu.VMEM((tps, seqs, widths[0]), bf16),
@@ -641,7 +702,7 @@
         widths = [x.shape[1] // tps for x in args[6:]]
         rows = args[6].shape[0]
         tiled = rows % 16 == 0 and all(width % 128 == 0 for width in widths)
-        tiled = tiled and rows > TAIL * 8 and rows * tps * sum(widths) % widths[1] == 0
+        tiled = tiled and rows > max(TAIL * 8, DETOUR) and rows * tps * sum(widths) % widths[1] == 0
         if reps % 4 or reps < 6 or tps != 4 or not tiled:
             return (per_device(*args[:6]), *native_move(*args[6:]))
         return tuple(flush(*fused(mesh, *args)))

time: 130 us -> 129 us (level); the launches traced: 128 us -> 129 us
  no operation moved by 1% of the time
where the time goes in v3:
time: 129 us
  Pallas kernels  128 us (99%)
    pallas_call x1, Pallas kernels, fused(): pl.pallas_call(functools.partial(step_kernel, planes, tps), out_shape=[pl...  123 us
    pallas_call x1, Pallas kernels, flush(): pl.pallas_call(flush_kernel, out_shape=[jax.ShapeDtypeStruct(x.shape, x.d...  5.18 us

profile of v3, /device:TPU:3, one launch (start us, length us, event | category | flops | bytes accessed | tf_op | source)
XLA Modules:
  0.0 128.7 jit_solution(2256082727097240174)
XLA Ops:
  0.6 122.9 %shard_map.112 = (bf16[4,896]{1,0:T(4,128)(2,1)S(1)}, bf16[3584,1152]{1,0:T(8,128)(2,1)S(1)}, bf16[3584,896]{1,0:T(8,128)(2,1)S(1)}) custom-call(bf16[4,3584]{1,0:T(4,128)(2,1)} %hidden_in.1, s32[4]{0:T(128)} %lengths_in.1, f32[1,128]{1,0:T(1,128)} %constant.2.clone.frequency_in, bf16[3584,1152]{1,0:T(8,128)(2,1)} %old_qkv.1, bf16[3584,896]{1,0:T(8,128)(2,1)} %old_out.1, ...), custom_call_target="tpu_custom_call" | custom-call | tf_op jit(solution)/shard_map/pallas_call | solution.py:674
  123.5 5.2 %shard_map.113 = (bf16[4,896]{1,0:T(4,128)(2,1)}, bf16[3584,1152]{1,0:T(8,128)(2,1)}, bf16[3584,896]{1,0:T(8,128)(2,1)}) custom-call(bf16[4,896]{1,0:T(4,128)(2,1)S(1)} %get-tuple-element.6.decoded, bf16[3584,1152]{1,0:T(8,128)(2,1)S(1)} %get-tuple-element.7.qkv, bf16[3584,896]{1,0:T(8,128)(2,1)S(1)} %get-tuple-element.8.out), custom_call_target="tpu_custom_call" | custom-call | tf_op jit(solution)/shard_map/pallas_call | solution.py:628

commit v4 on v3

--- a/solution.py
+++ b/solution.py
@@ -12,7 +12,7 @@
 KVH = 4
 HD = 128
 PAD = 8
-CUTS = 28
+CUTS = 56
 TAIL = 4
 DETOUR = 16
 VMEM_BYTES = 67043328
@@ -113,10 +113,9 @@
     planes, tps,
     hidden_in, lengths_in, frequency_in, old_qkv, old_out, keys, values, new_qkv, new_out,
     decoded, qkv_full, out_full,
-    a_send, a_recv, z_send, z_recv, z_last, s_send, s_recv, t_send, t_recv, own_sem,
-    load_sem, small_sem, met, d_send, d_recv,
+    a_recv, z_send, z_recv, s_send, s_recv, t_recv, x_recv, local, met,
     stage, detour,
-    w_qkv, w_out, k_held, v_held, joined, rotated, own_score, own_value, parts, attended,
+    weights, caches, joined, rotated, own_score, own_value, parts, attended,
     cosine, sine, hidden, frequency, lengths,
 ):
     rep, tp = lax.axis_index("rep"), lax.axis_index("tp")
@@ -145,17 +144,17 @@
     mine = [
         pltpu.make_async_copy(
             source.at[:, pl.ds(pl.multiple_of(tp * widths[w], 128), widths[w])],
-            piece_rows(plane, core, 0, w), own_sem.at[w],
+            piece_rows(plane, core, 0, w), local.at[w],
         )
         for w, source in enumerate((new_qkv, new_out))
     ]
     staged = [
         pltpu.make_async_copy(
-            source, stage.at[:, pl.ds(bases[w], source.shape[1])], own_sem.at[2 + w]
+            source, stage.at[:, pl.ds(bases[w], source.shape[1])], local.at[2]
         )
         for w, source in enumerate((new_qkv, new_out))
     ]
-    for copy in mine + staged:
+    for copy in mine:
         copy.start()
     barrier = pltpu.get_barrier_semaphore()
     beside = [twin] + [peers[k - 1] for k in near]
@@ -175,9 +174,11 @@
     def _():
         for device in beside:
             tell(barrier, device)
+        for copy in staged:
+            copy.start()
 
     small = [
-        pltpu.make_async_copy(source, target, load_sem.at[4 + i])
+        pltpu.make_async_copy(source, target, local.at[i])
         for i, (source, target) in enumerate(
             ((hidden_in, hidden), (frequency_in, frequency), (lengths_in, lengths))
         )
@@ -217,36 +218,31 @@
     def parts_of(h, last):
         if last and h == half - 1:
             return [(0, 0, 2 * rows, 0), (1, 0, 2 * rows - tail, 1)]
-        return [(w, 0, 2 * rows, None) for w in range(2)]
+        return [(w, 0, 2 * rows, 0) for w in range(2)]
 
     def part_rows(source_plane, source_core, h, part):
         w, first, count = part[:3]
         return at_rows(source_plane, source_core, pair_first(h) + first, count, w)
 
-    def part_sem(source_plane, h, part):
-        return z_recv.at[source_plane, h] if part[3] is None else z_last.at[part[3]]
+    def part_sem(index, h, part):
+        return x_recv.at[0] if part[3] else z_recv.at[index, h]
 
     def bytes_of(parts):
         return stage.at[:, pl.ds(0, stage.shape[1] // tps * parts)]
 
     def out_rows(count):
         return out_full.at[pl.ds(0, count)]
-
-    def block_bytes(last):
-        if last:
-            return out_rows(rows * tps * sum(widths) // widths[1] - tail)
-        return stage
 
     def send_tails(source_plane, device):
         for i, (c, part) in enumerate(tails):
             ref = part_rows(source_plane, c, half - 1, part)
-            remote(ref, ref, t_send.at[0], t_recv.at[i], device).start()
+            remote(ref, ref, local.at[6], t_recv.at[i], device).start()
 
     def take_tails(source_plane):
         for i, (c, part) in enumerate(tails):
             ref = part_rows(source_plane, c, half - 1, part)
             landed(ref, t_recv.at[i])
-            remote(ref, ref, t_send.at[1], t_recv.at[len(tails)], twin).start()
+            remote(ref, ref, local.at[6], t_recv.at[len(tails)], twin).start()
 
     def column(w, t):
         start = bases[w] + t * widths[w]
@@ -255,7 +251,7 @@
     def in_plane(k, w):
         remote(
             column(w, flip(tp, k, tps)), piece_rows(plane, core, 0, w),
-            a_send.at[0], a_recv.at[k - 1, w], peers[k - 1],
+            local.at[5], a_recv.at[k - 1, w], peers[k - 1],
         ).start()
 
     def own_up(k, w):
@@ -263,13 +259,13 @@
 
         @pl.when(can_up)
         def _():
-            remote(ref, ref, z_send.at[plane], z_recv.at[plane, k // 2], up).start()
+            remote(ref, ref, z_send.at[0], z_recv.at[plane, k // 2], up).start()
 
     def own_down(k, w):
         ref = piece_rows(plane, core, k, w)
 
         def send(ref):
-            remote(ref, ref, z_send.at[plane + 1], z_recv.at[plane, k // 2], down).start()
+            remote(ref, ref, z_send.at[1], z_recv.at[plane - 1, k // 2], down).start()
 
         if w and k:
             short = detoured & (core == (k + 1) % 2)
@@ -290,7 +286,7 @@
 
     def own_twin(k, w):
         ref = piece_rows(plane, core, k, w)
-        remote(ref, ref, s_send.at[plane], s_recv.at[plane], twin).start()
+        remote(ref, ref, s_send.at[0], s_recv.at[0], twin).start()
 
     detoured = (plane == 1) & (tp == 0)
     carries = (tp != 0) & (core == (tp + 1) % 2)
@@ -299,110 +295,96 @@
         @pl.when((plane == 1) & carries)
         def _():
             source = stage.at[pl.ds(rows - DETOUR, DETOUR), pl.ds(bases[1], widths[1])]
-            remote(source, detour, d_send.at[0], d_recv.at[0], down).start()
+            remote(source, detour, local.at[6], x_recv.at[1], down).start()
 
     def detour_across():
         @pl.when((plane == 0) & carries)
         def _():
-            landed(detour, d_recv.at[0])
+            landed(detour, x_recv.at[1])
             target = at_rows(1, core, tp * rows + rows - DETOUR, DETOUR, 1)
-            remote(detour, target, d_send.at[0], z_recv.at[1, tp // 2], (rep, jnp.int32(0))).start()
-
-    def take(source_plane, h, last, parts, forward, slot, onward):
-        if last:
+            remote(detour, target, local.at[6], z_recv.at[0, tp // 2], (rep, jnp.int32(0))).start()
+
+    def take(source_plane, index, h, single, parts, far, can, device, way, onward):
+        if single:
             (part,) = parts
-            landed(part_rows(source_plane, core, h, part), part_sem(source_plane, h, part))
+            landed(part_rows(source_plane, core, h, part), part_sem(index, h, part))
         else:
-            landed(bytes_of(2), z_recv.at[source_plane, h])
-        if forward is not None:
-            can, device = forward
+            landed(bytes_of(2), z_recv.at[index, h])
+        if onward:
 
             @pl.when(can)
             def _():
                 for part in onward:
                     ref = part_rows(source_plane, core, h, part)
-                    remote(
-                        ref, ref, z_send.at[slot], part_sem(source_plane, h, part), device
-                    ).start()
+                    sem = part_sem(source_plane - way, h, part)
+                    remote(ref, ref, z_send.at[way], sem, device).start()
 
         for part in parts:
             ref = part_rows(source_plane, core, h, part)
-            remote(ref, ref, s_send.at[source_plane], s_recv.at[source_plane], twin).start()
+            remote(ref, ref, s_send.at[far], s_recv.at[far], twin).start()
+
+    def farthest(source_plane):
+        other = jnp.where(plane < planes // 2, planes - 1, 0)
+        return jnp.where(source_plane == other, 1, 0)
 
     def relay(d):
         ends = d == planes - 1
         for h in range(half):
             cuts = parts_of(h, ends)
-            onward = parts_of(h, d == planes - 2)
+            onward = [] if ends else parts_of(h, d == planes - 2)
             single = ends and h == half - 1
             for parts in [[part] for part in cuts] if single else [cuts]:
 
                 @pl.when(plane >= d)
                 def _():
-                    take(plane - d, h, single, parts, None if ends else (can_up, up), plane - d, onward)
+                    s = plane - d
+                    take(s, s, h, single, parts, farthest(s), can_up, up, 0, onward)
 
                 @pl.when(plane + d < planes)
                 def _():
-                    take(
-                        plane + d, h, single, parts,
-                        None if ends else (can_down, down), plane + d + 1, onward,
-                    )
-
-    def settle_twin(source_plane, last):
-        landed(block_bytes(last), s_recv.at[source_plane])
-        sent(block_bytes(last), s_send.at[source_plane])
-
-    def settle_own():
-        cut = rows * tps * sum(widths) // widths[1]
-        shorts = [
-            (c, cut - DETOUR * sum((k + 1) % 2 == c for k in range(1, tps))) for c in range(2)
-        ]
-
-        @pl.when(can_up)
+                    s = plane + d
+                    take(s, s - 1, h, single, parts, farthest(s), can_down, down, 1, onward)
+
+    block = rows * tps * sum(widths) // widths[1]
+
+    def settle_twin(count, far):
+        landed(out_rows(count), s_recv.at[far])
+        sent(out_rows(count), s_send.at[far])
+
+    def settle_next(p):
+        @pl.when(plane == p)
         def _():
-            sent(stage, z_send.at[plane])
-
-        @pl.when(can_down & jnp.logical_not(detoured))
-        def _():
-            sent(stage, z_send.at[plane + 1])
-
-        for c, count in shorts:
-
-            @pl.when(detoured & (core == c))
-            def _():
-                sent(out_rows(count), z_send.at[plane + 1])
-
-        @pl.when((plane < 2) & carries)
-        def _():
-            sent(detour, d_send.at[0])
-
-    def settle_next(d):
-        @pl.when((plane >= d) & can_up)
-        def _():
-            sent(block_bytes(d == planes - 2), z_send.at[plane - d])
-
-        @pl.when((plane + d < planes) & can_down)
-        def _():
-            sent(block_bytes(d == planes - 2), z_send.at[plane + d + 1])
-
-    def settle(d):
-        @pl.when(plane >= d)
-        def _():
-            settle_twin(plane - d, d == planes - 1)
-
-        if d:
-
-            @pl.when(plane + d < planes)
-            def _():
-                settle_twin(plane + d, d == planes - 1)
+            for way, count in ((0, p + 1), (1, planes - p)):
+                if p == (planes - 1, 0)[way]:
+                    continue
+                total = count * block - (tail if p == (planes - 2, 1)[way] else 0)
+                if p != 1 or way == 0:
+                    sent(out_rows(total), z_send.at[way])
+                    continue
+
+                @pl.when(tp != 0)
+                def _():
+                    sent(out_rows(total), z_send.at[way])
+
+                for c in range(2):
+                    cut = DETOUR * sum((k + 1) % 2 == c for k in range(1, tps))
+
+                    @pl.when((tp == 0) & (core == c))
+                    def _():
+                        sent(out_rows(total - cut), z_send.at[way])
 
     for w in range(2):
         mine[w].wait()
         own_down(0, w)
 
+    @pl.when(plane == 1)
+    def _():
+        for copy in staged:
+            copy.start()
+
     def open_plane():
+        pltpu.make_async_copy(stage, stage, local.at[2]).wait()
         for w in (1, 0):
-            staged[w].wait()
             for k in near:
                 in_plane(k, w)
         for w in range(2):
@@ -426,22 +408,25 @@
     @pl.when(plane == 0)
     def _():
         pl.semaphore_wait(met.at[0], len(beside))
-        tell(met.at[2], up)
+        tell(met.at[0], up)
 
     @pl.when(plane == 1)
     def _():
-        pl.semaphore_wait(met.at[2], 1)
+        pl.semaphore_wait(met.at[0], 1)
         open_plane()
         detour_down()
         pl.semaphore_wait(met.at[1], 1)
         for w in range(2):
             own_up(0, w)
 
+    held = [caches.at[i] for i in range(2)]
     loads = [
-        pltpu.make_async_copy(source, target, load_sem.at[i])
-        for i, (source, target) in enumerate(
-            ((old_qkv, w_qkv), (keys, k_held), (values, v_held), (old_out, w_out))
+        pltpu.make_async_copy(source, target, local.at[3 + i])
+        for sources, targets, i in (
+            ((old_qkv, old_out), [weights.at[:, pl.ds(sum(widths[:w]), widths[w])] for w in range(2)], 0),
+            ((keys, values), held, 1),
         )
+        for source, target in zip(sources, targets)
     ]
     for copy in loads + small:
         copy.start()
@@ -466,29 +451,28 @@
         cosine[s : s + 1, :] = jnp.cos(angles)
         sine[s : s + 1, :] = jnp.where(lane < HD // 2, -jnp.sin(angles), jnp.sin(angles))
     tile = 128
-    loads[0].wait()
-
-    @pl.loop(0, w_qkv.shape[1] // tile)
+    pltpu.make_async_copy(weights, weights, local.at[3]).wait()
+    pltpu.make_async_copy(caches, caches, local.at[4]).wait()
+
+    @pl.loop(0, widths[0] // tile)
     def _(i):
         at = pl.ds(pl.multiple_of(i * tile, tile), tile)
         joined[tp, :, at] = jnp.dot(
-            hidden[...], w_qkv[:, at], preferred_element_type=jnp.float32
+            hidden[...], weights[:, at], preferred_element_type=jnp.float32
         ).astype(joined.dtype)
 
     def send_all(ref, send, recv):
         for k in range(1, tps):
             remote(ref.at[tp], ref.at[tp], send, recv, peers[k - 1]).start()
 
-    send_all(joined, small_sem.at[0], small_sem.at[1])
+    send_all(joined, local.at[0], x_recv.at[2])
 
     relay(1)
 
-    landed(joined.at[pl.ds(0, tps - 1)], small_sem.at[1])
-    for copy in loads[1:]:
-        copy.wait()
+    landed(joined.at[pl.ds(0, tps - 1)], x_recv.at[2])
 
     group = HQ // KVH
-    positions = k_held.shape[1]
+    positions = caches.shape[2]
     per_slot = joined.shape[2] // HD
     inv_root = 1.0 / jnp.sqrt(jnp.float32(HD))
 
@@ -522,24 +506,30 @@
             lanes = slice(kv * PAD, (kv + 1) * PAD)
             query = rotated[s, lanes, :].astype(jnp.bfloat16)
             scores = lax.dot_general(
-                query, k_held[s, :, at], (((1,), (1,)), ((), ())),
+                query, caches[0, s, :, at], (((1,), (1,)), ((), ())),
                 preferred_element_type=jnp.float32,
             ) * inv_root
             scores = jnp.where(is_live, scores, jnp.float32(-1e30))
             top = jnp.max(scores, axis=1, keepdims=True)
-            weights = jnp.where(is_live, jnp.exp(scores - top), 0.0).astype(jnp.bfloat16)
-            total = jnp.sum(weights.astype(jnp.float32), axis=1, keepdims=True)
+            shares = jnp.where(is_live, jnp.exp(scores - top), 0.0).astype(jnp.bfloat16)
+            total = jnp.sum(shares.astype(jnp.float32), axis=1, keepdims=True)
             parts[tp, 0, s, lanes, :] = jnp.dot(
-                weights, v_held[s, :, at], preferred_element_type=jnp.float32
+                shares, caches[1, s, :, at], preferred_element_type=jnp.float32
             )
             parts[tp, 1, s, lanes, :] = jnp.broadcast_to(top, (PAD, HD))
             parts[tp, 2, s, lanes, :] = jnp.broadcast_to(total, (PAD, HD))
 
-    send_all(parts, small_sem.at[2], small_sem.at[3])
+    send_all(parts, local.at[1], x_recv.at[3])
 
     for d in range(2, planes - 1):
         relay(d)
-    settle(planes - 2)
+    @pl.when((plane < 2) & carries)
+    def _():
+        sent(detour, local.at[6])
+
+    @pl.when((plane == 1) | (plane == planes - 2))
+    def _():
+        settle_twin(block, 1)
 
     @pl.when((core == 1) & (plane == planes - 2))
     def _():
@@ -550,7 +540,7 @@
         send_tails(planes - 1, down)
 
 
-    landed(parts.at[pl.ds(0, tps - 1)], small_sem.at[3])
+    landed(parts.at[pl.ds(0, tps - 1)], x_recv.at[3])
 
     @pl.loop(0, seqs)
     def _(s):
@@ -570,19 +560,21 @@
         row = (j // group) * PAD + j % group
         attended[:, j * HD : (j + 1) * HD] = rotated[:, row, :].astype(attended.dtype)
 
-    @pl.loop(0, w_out.shape[1] // tile)
+    @pl.loop(0, widths[1] // tile)
     def _(i):
         at = pl.ds(pl.multiple_of(i * tile, tile), tile)
+        under = pl.ds(pl.multiple_of(widths[0] + i * tile, tile), tile)
         decoded[:, at] = jnp.dot(
-            attended[...], w_out[:, at], preferred_element_type=jnp.float32
+            attended[...], weights[:, under], preferred_element_type=jnp.float32
         ).astype(decoded.dtype)
 
-    sent(bytes_of(tps - 1), a_send.at[0])
-    sent(joined.at[pl.ds(0, tps - 1)], small_sem.at[0])
-    sent(parts.at[pl.ds(0, tps - 1)], small_sem.at[2])
-    for d in range(planes - 2):
-        settle(d)
-    settle_own()
+    sent(bytes_of(tps - 1), local.at[5])
+    sent(joined.at[pl.ds(0, tps - 1)], local.at[0])
+    sent(parts.at[pl.ds(0, tps - 1)], local.at[1])
+    settle_twin((planes - 1) * block, 0)
+    settle_next(0)
+    settle_next(planes - 1)
+    at_end = (plane == 0) | (plane == planes - 1)
     relay(planes - 1)
 
     @pl.when((core == 1) & (plane == planes - 1))
@@ -593,23 +585,20 @@
     def _():
         take_tails(planes - 1)
 
-    settle(planes - 1)
-    at_end = (plane == 0) | (plane == planes - 1)
-
-    @pl.when(at_end & (core == 1))
-    def _():
-        sent(out_rows(2 * tail), t_send.at[1])
+    @pl.when(at_end)
+    def _():
+        settle_twin(block - tail, 1)
 
     @pl.when(at_end & (core == 0))
     def _():
         landed(out_rows(2 * tail), t_recv.at[len(tails)])
 
-    for d in range(1, planes - 1):
-        settle_next(d)
-
-    @pl.when((core == 1) & ((plane == 1) | (plane == planes - 2)))
-    def _():
-        sent(out_rows(2 * tail), t_send.at[0])
+    for p in range(1, planes - 1):
+        settle_next(p)
+
+    @pl.when((core == 1) & (at_end | (plane == 1) | (plane == planes - 2)))
+    def _():
+        sent(out_rows(2 * tail), local.at[6])
 
 
 def flush_kernel(decoded, qkv, out, decoded_to, qkv_to, out_to, sems):
@@ -651,13 +640,11 @@
     f32, bf16 = jnp.float32, jnp.bfloat16
     padded = KVH * PAD
     landed = 2 * rows * reps * tps * sum(widths)
-    scratch = [sem((1,)), sem((tps - 1, 2)), sem((planes + 1,)), sem((planes, tps // 2)), sem((2,))]
-    scratch += [sem((planes,)), sem((planes,)), sem((2,)), sem((5,))]
-    scratch += [sem((4,)), sem((7,)), sem((4,)), pltpu.SemaphoreType.REGULAR((3,))]
-    scratch += [sem((1,)), sem((1,))]
+    scratch = [sem((tps - 1, 2)), sem((2,)), sem((planes - 1, tps // 2)), sem((2,)), sem((2,))]
+    scratch += [sem((5,)), sem((4,)), sem((7,)), pltpu.SemaphoreType.REGULAR((2,))]
     scratch += [pltpu.VMEM((rows, new_qkv.shape[1] + new_out.shape[1]), bf16)]
     scratch += [pltpu.VMEM((DETOUR, widths[1]), bf16)]
-    scratch += [pltpu.VMEM(x.shape, x.dtype) for x in (old_qkv, old_out, keys, values)]
+    scratch += [pltpu.VMEM((old_qkv.shape[0], sum(widths)), bf16), pltpu.VMEM((2, *keys.shape), bf16)]
     scratch += [
         pltpu.VMEM((tps, seqs, widths[0]), bf16),
         pltpu.VMEM((seqs, padded, HD), f32),
@@ -703,6 +690,7 @@
         rows = args[6].shape[0]
         tiled = rows % 16 == 0 and all(width % 128 == 0 for width in widths)
         tiled = tiled and rows > max(TAIL * 8, DETOUR) and rows * tps * sum(widths) % widths[1] == 0
+        tiled = tiled and args[2].shape[0] == args[3].shape[0]
         if reps % 4 or reps < 6 or tps != 4 or not tiled:
             return (per_device(*args[:6]), *native_move(*args[6:]))
         return tuple(flush(*fused(mesh, *args)))

time: 129 us -> 129 us (level)
  no operation moved by 1% of the time
where the time goes in v4:
time: 129 us
  Pallas kernels  128 us (99%)
    pallas_call x1, Pallas kernels, fused(): pl.pallas_call(functools.partial(step_kernel, planes, tps), out_shape=[pl...  123 us
    pallas_call x1, Pallas kernels, flush(): pl.pallas_call(flush_kernel, out_shape=[jax.ShapeDtypeStruct(x.shape, x.d...  5.16 us

profile of v4, /device:TPU:3, one launch (start us, length us, event | category | flops | bytes accessed | tf_op | source)
XLA Modules:
  0.0 128.5 jit_solution(378613074488211900)
XLA Ops:
  0.6 122.7 %shard_map.112 = (bf16[4,896]{1,0:T(4,128)(2,1)S(1)}, bf16[3584,1152]{1,0:T(8,128)(2,1)S(1)}, bf16[3584,896]{1,0:T(8,128)(2,1)S(1)}) custom-call(bf16[4,3584]{1,0:T(4,128)(2,1)} %hidden_in.1, s32[4]{0:T(128)} %lengths_in.1, f32[1,128]{1,0:T(1,128)} %constant.2.clone.frequency_in, bf16[3584,1152]{1,0:T(8,128)(2,1)} %old_qkv.1, bf16[3584,896]{1,0:T(8,128)(2,1)} %old_out.1, ...), custom_call_target="tpu_custom_call" | custom-call | tf_op jit(solution)/shard_map/pallas_call | solution.py:661
  123.3 5.2 %shard_map.113 = (bf16[4,896]{1,0:T(4,128)(2,1)}, bf16[3584,1152]{1,0:T(8,128)(2,1)}, bf16[3584,896]{1,0:T(8,128)(2,1)}) custom-call(bf16[4,896]{1,0:T(4,128)(2,1)S(1)} %get-tuple-element.6.decoded, bf16[3584,1152]{1,0:T(8,128)(2,1)S(1)} %get-tuple-element.7.qkv, bf16[3584,896]{1,0:T(8,128)(2,1)S(1)} %get-tuple-element.8.out), custom_call_target="tpu_custom_call" | custom-call | tf_op jit(solution)/shard_map/pallas_call | solution.py:617

commit v5 on v4

--- a/solution.py
+++ b/solution.py
@@ -154,8 +154,6 @@
         )
         for w, source in enumerate((new_qkv, new_out))
     ]
-    for copy in mine:
-        copy.start()
     barrier = pltpu.get_barrier_semaphore()
     beside = [twin] + [peers[k - 1] for k in near]
 
@@ -174,7 +172,7 @@
     def _():
         for device in beside:
             tell(barrier, device)
-        for copy in staged:
+        for copy in mine + staged:
             copy.start()
 
     small = [
@@ -373,14 +371,23 @@
                     def _():
                         sent(out_rows(total - cut), z_send.at[way])
 
+    @pl.when(plane == 1)
+    def _():
+        for w, source in enumerate((new_qkv, new_out)):
+            columns = pl.ds(pl.multiple_of(tp * widths[w], 128), widths[w])
+            remote(
+                source.at[:, columns], piece_rows(plane, core, 0, w),
+                z_send.at[1], z_recv.at[plane - 1, 0], down,
+            ).start()
+        for copy in mine + staged:
+            copy.start()
+
     for w in range(2):
         mine[w].wait()
-        own_down(0, w)
-
-    @pl.when(plane == 1)
-    def _():
-        for copy in staged:
-            copy.start()
+
+        @pl.when(plane != 1)
+        def _():
+            own_down(0, w)
 
     def open_plane():
         pltpu.make_async_copy(stage, stage, local.at[2]).wait()

time: 129 us -> 128 us (level)
  no operation moved by 1% of the time
where the time goes in v5:
time: 128 us
  Pallas kernels  127 us (99%)
    pallas_call x1, Pallas kernels, fused(): pl.pallas_call(functools.partial(step_kernel, planes, tps), out_shape=[pl...  122 us
    pallas_call x1, Pallas kernels, flush(): pl.pallas_call(flush_kernel, out_shape=[jax.ShapeDtypeStruct(x.shape, x.d...  5.16 us

profile of v5, /device:TPU:3, one launch (start us, length us, event | category | flops | bytes accessed | tf_op | source)
XLA Modules:
  0.0 127.9 jit_solution(115909995642111794)
XLA Ops:
  0.6 122.1 %shard_map.112 = (bf16[4,896]{1,0:T(4,128)(2,1)S(1)}, bf16[3584,1152]{1,0:T(8,128)(2,1)S(1)}, bf16[3584,896]{1,0:T(8,128)(2,1)S(1)}) custom-call(bf16[4,3584]{1,0:T(4,128)(2,1)} %hidden_in.1, s32[4]{0:T(128)} %lengths_in.1, f32[1,128]{1,0:T(1,128)} %constant.2.clone.frequency_in, bf16[3584,1152]{1,0:T(8,128)(2,1)} %old_qkv.1, bf16[3584,896]{1,0:T(8,128)(2,1)} %old_out.1, ...), custom_call_target="tpu_custom_call" | custom-call | tf_op jit(solution)/shard_map/pallas_call | solution.py:668
  122.8 5.2 %shard_map.113 = (bf16[4,896]{1,0:T(4,128)(2,1)}, bf16[3584,1152]{1,0:T(8,128)(2,1)}, bf16[3584,896]{1,0:T(8,128)(2,1)}) custom-call(bf16[4,896]{1,0:T(4,128)(2,1)S(1)} %get-tuple-element.6.decoded, bf16[3584,1152]{1,0:T(8,128)(2,1)S(1)} %get-tuple-element.7.qkv, bf16[3584,896]{1,0:T(8,128)(2,1)S(1)} %get-tuple-element.8.out), custom_call_target="tpu_custom_call" | custom-call | tf_op jit(solution)/shard_map/pallas_call | solution.py:624

commit v6 on v5

--- a/solution.py
+++ b/solution.py
@@ -234,13 +234,17 @@
     def send_tails(source_plane, device):
         for i, (c, part) in enumerate(tails):
             ref = part_rows(source_plane, c, half - 1, part)
+            if i == len(tails) - 1:
+                other = (device[0] - 1, tp)
+                remote(ref, ref, local.at[6], t_recv.at[len(tails)], other).start()
             remote(ref, ref, local.at[6], t_recv.at[i], device).start()
 
     def take_tails(source_plane):
         for i, (c, part) in enumerate(tails):
             ref = part_rows(source_plane, c, half - 1, part)
             landed(ref, t_recv.at[i])
-            remote(ref, ref, local.at[6], t_recv.at[len(tails)], twin).start()
+            if i < len(tails) - 1:
+                remote(ref, ref, local.at[6], t_recv.at[len(tails)], twin).start()
 
     def column(w, t):
         start = bases[w] + t * widths[w]
@@ -603,9 +607,13 @@
     for p in range(1, planes - 1):
         settle_next(p)
 
-    @pl.when((core == 1) & (at_end | (plane == 1) | (plane == planes - 2)))
-    def _():
-        sent(out_rows(2 * tail), local.at[6])
+    @pl.when((core == 1) & at_end)
+    def _():
+        sent(out_rows(2 * tail - 16), local.at[6])
+
+    @pl.when((core == 1) & ((plane == 1) | (plane == planes - 2)))
+    def _():
+        sent(out_rows(2 * tail + 16), local.at[6])
 
 
 def flush_kernel(decoded, qkv, out, decoded_to, qkv_to, out_to, sems):

time: 128 us -> 128 us (level)
  no operation moved by 1% of the time
where the time goes in v6:
time: 128 us
  Pallas kernels  127 us (99%)
    pallas_call x1, Pallas kernels, fused(): pl.pallas_call(functools.partial(step_kernel, planes, tps), out_shape=[pl...  122 us
    pallas_call x1, Pallas kernels, flush(): pl.pallas_call(flush_kernel, out_shape=[jax.ShapeDtypeStruct(x.shape, x.d...  5.16 us

profile of v6, /device:TPU:3, one launch (start us, length us, event | category | flops | bytes accessed | tf_op | source)
XLA Modules:
  0.0 127.8 jit_solution(2120198974042184456)
XLA Ops:
  0.6 122.0 %shard_map.112 = (bf16[4,896]{1,0:T(4,128)(2,1)S(1)}, bf16[3584,1152]{1,0:T(8,128)(2,1)S(1)}, bf16[3584,896]{1,0:T(8,128)(2,1)S(1)}) custom-call(bf16[4,3584]{1,0:T(4,128)(2,1)} %hidden_in.1, s32[4]{0:T(128)} %lengths_in.1, f32[1,128]{1,0:T(1,128)} %constant.2.clone.frequency_in, bf16[3584,1152]{1,0:T(8,128)(2,1)} %old_qkv.1, bf16[3584,896]{1,0:T(8,128)(2,1)} %old_out.1, ...), custom_call_target="tpu_custom_call" | custom-call | tf_op jit(solution)/shard_map/pallas_call | solution.py:676
  122.7 5.2 %shard_map.113 = (bf16[4,896]{1,0:T(4,128)(2,1)}, bf16[3584,1152]{1,0:T(8,128)(2,1)}, bf16[3584,896]{1,0:T(8,128)(2,1)}) custom-call(bf16[4,896]{1,0:T(4,128)(2,1)S(1)} %get-tuple-element.6.decoded, bf16[3584,1152]{1,0:T(8,128)(2,1)S(1)} %get-tuple-element.7.qkv, bf16[3584,896]{1,0:T(8,128)(2,1)S(1)} %get-tuple-element.8.out), custom_call_target="tpu_custom_call" | custom-call | tf_op jit(solution)/shard_map/pallas_call | solution.py:632

commit v7 on v6

--- a/solution.py
+++ b/solution.py
@@ -215,7 +215,8 @@
 
     def parts_of(h, last):
         if last and h == half - 1:
-            return [(0, 0, 2 * rows, 0), (1, 0, 2 * rows - tail, 1)]
+            first = 2 * rows - 2 * tail
+            return [(0, 0, 2 * rows, 0), (1, 0, first, 1), (1, first, tail, 2)]
         return [(w, 0, 2 * rows, 0) for w in range(2)]
 
     def part_rows(source_plane, source_core, h, part):
@@ -223,7 +224,7 @@
         return at_rows(source_plane, source_core, pair_first(h) + first, count, w)
 
     def part_sem(index, h, part):
-        return x_recv.at[0] if part[3] else z_recv.at[index, h]
+        return x_recv.at[(part[3] - 1) * 4] if part[3] else z_recv.at[index, h]
 
     def bytes_of(parts):
         return stage.at[:, pl.ds(0, stage.shape[1] // tps * parts)]
@@ -656,7 +657,7 @@
     padded = KVH * PAD
     landed = 2 * rows * reps * tps * sum(widths)
     scratch = [sem((tps - 1, 2)), sem((2,)), sem((planes - 1, tps // 2)), sem((2,)), sem((2,))]
-    scratch += [sem((5,)), sem((4,)), sem((7,)), pltpu.SemaphoreType.REGULAR((2,))]
+    scratch += [sem((5,)), sem((5,)), sem((7,)), pltpu.SemaphoreType.REGULAR((2,))]
     scratch += [pltpu.VMEM((rows, new_qkv.shape[1] + new_out.shape[1]), bf16)]
     scratch += [pltpu.VMEM((DETOUR, widths[1]), bf16)]
     scratch += [pltpu.VMEM((old_qkv.shape[0], sum(widths)), bf16), pltpu.VMEM((2, *keys.shape), bf16)]
@@ -704,7 +705,7 @@
         widths = [x.shape[1] // tps for x in args[6:]]
         rows = args[6].shape[0]
         tiled = rows % 16 == 0 and all(width % 128 == 0 for width in widths)
-        tiled = tiled and rows > max(TAIL * 8, DETOUR) and rows * tps * sum(widths) % widths[1] == 0
+        tiled = tiled and rows > max(TAIL * 16, DETOUR) and rows * tps * sum(widths) % widths[1] == 0
         tiled = tiled and args[2].shape[0] == args[3].shape[0]
         if reps % 4 or reps < 6 or tps != 4 or not tiled:
             return (per_device(*args[:6]), *native_move(*args[6:]))

time: 128 us -> 128 us (level)
  no operation moved by 1% of the time
where the time goes in v7:
time: 128 us
  Pallas kernels  127 us (99%)
    pallas_call x1, Pallas kernels, fused(): pl.pallas_call(functools.partial(step_kernel, planes, tps), out_shape=[pl...  122 us
    pallas_call x1, Pallas kernels, flush(): pl.pallas_call(flush_kernel, out_shape=[jax.ShapeDtypeStruct(x.shape, x.d...  5.16 us

profile of v7, /device:TPU:3, one launch (start us, length us, event | category | flops | bytes accessed | tf_op | source)
XLA Modules:
  0.0 127.6 jit_solution(1570996686874480575)
XLA Ops:
  0.6 121.8 %shard_map.112 = (bf16[4,896]{1,0:T(4,128)(2,1)S(1)}, bf16[3584,1152]{1,0:T(8,128)(2,1)S(1)}, bf16[3584,896]{1,0:T(8,128)(2,1)S(1)}) custom-call(bf16[4,3584]{1,0:T(4,128)(2,1)} %hidden_in.1, s32[4]{0:T(128)} %lengths_in.1, f32[1,128]{1,0:T(1,128)} %constant.2.clone.frequency_in, bf16[3584,1152]{1,0:T(8,128)(2,1)} %old_qkv.1, bf16[3584,896]{1,0:T(8,128)(2,1)} %old_out.1, ...), custom_call_target="tpu_custom_call" | custom-call | tf_op jit(solution)/shard_map/pallas_call | solution.py:677
  122.5 5.2 %shard_map.113 = (bf16[4,896]{1,0:T(4,128)(2,1)}, bf16[3584,1152]{1,0:T(8,128)(2,1)}, bf16[3584,896]{1,0:T(8,128)(2,1)}) custom-call(bf16[4,896]{1,0:T(4,128)(2,1)S(1)} %get-tuple-element.6.decoded, bf16[3584,1152]{1,0:T(8,128)(2,1)S(1)} %get-tuple-element.7.qkv, bf16[3584,896]{1,0:T(8,128)(2,1)S(1)} %get-tuple-element.8.out), custom_call_target="tpu_custom_call" | custom-call | tf_op jit(solution)/shard_map/pallas_call | solution.py:633
